TPU v7x, 256 devices: a whole 4x4x8 slice. The times are simulated.
256 devices in a mesh: grp: 16 (over z, core), tp: 16 (over y, x).
Axes of the slice: x: 4, y: 4, z: 8, core: 2. Of those that a mesh axis runs over, the one named last changes fastest.
Arguments:
- window_queries: bfloat16 [512, 16384], P('grp', 'tp'), parts along dimension 0, may hold values from -64 to 64
- key_rows: bfloat16 [16, 262144, 128], P('tp', 'grp'), parts along dimension 1, may hold values from -16 to 16
- value_rows: bfloat16 [16, 262144, 128], P('tp', 'grp'), parts along dimension 1, may hold values from -6 to 6
- kept: int32 [8, 32768], P(None, 'grp'), parts along dimension 1, may hold values from 0 to 32735, as said below
Outputs:
- window_out: bfloat16 [512, 16384], P('grp', 'tp'), parts along dimension 0
- kept_keys: bfloat16 [16, 8, 4096, 128], P('tp', None, 'grp'), parts along dimension 2
- kept_values: bfloat16 [16, 8, 4096, 128], P('tp', None, 'grp'), parts along dimension 2
- kept_votes: bfloat16 [16, 128, 256], P('tp', 'grp'), parts along dimension 1
There are 16 independent parts, one for each index of `grp`. A program takes and returns all parts, laid end to end along the dimension named above; each array names one. Nothing has to cross between parts.
Inputs may be any that keep to these rules, and one draw needn't show every extreme that they name: `kept`: each row lists 2048 distinct positions in ascending order, all below 32736; the first 1024 lie below 16384, the rest at or above it. For every head and half, at most 128 of its positions belong to one owner (owner (p // 128) mod 16), and some owner gets exactly 128.
All inputs are finite; a program needn't handle non-finite values.
Results may differ from a plain program's by a relative error of at most 0.005.
Values may be sent and summed in bfloat16 or wider, within the bound.
A program may use at most 128 MiB of HBM per device.

v0:
```python
import math

import jax
import jax.numpy as jnp
from jax import lax
from jax.sharding import PartitionSpec as P

HQ = 128
KVH = 8
SEQ = 32768
WIN = 32
OWNER_BLOCK = 128


masked_score = -1e30


def partner(value, axis, distance):
    mask = 2**distance
    pairs = [(source, source ^ mask) for source in range(lax.axis_size(axis))]
    return lax.ppermute(value, axis, pairs)


def in_one_piece(arrays, axis, split_dim, concat_dim, along):
    widths = [math.prod(a.shape[along:]) for a in arrays]
    both = jnp.concatenate(
        [a.reshape(*a.shape[:along], w) for a, w in zip(arrays, widths)], axis=along
    )
    out = lax.all_to_all(both, axis, split_axis=split_dim, concat_axis=concat_dim, tiled=True)
    blocks = jnp.split(out, [sum(widths[:k]) for k in range(1, len(widths))], axis=along)
    return tuple((b.reshape(*out.shape[:along], *a.shape[along:]) for a, b in zip(arrays, blocks)))


def block_length():
    return 2048


def scores_of(queries, key_block, start):
    scale = queries.shape[-1] ** (-0.5)
    raw = jnp.einsum("hwd,pd->hwp", queries, key_block, preferred_element_type=jnp.float32) * scale
    window = queries.shape[1]
    query_pos = SEQ - window + lax.broadcasted_iota(jnp.int32, (1, window, 1), 1)
    key_pos = start + lax.broadcasted_iota(jnp.int32, (1, 1, key_block.shape[0]), 2)
    return (jnp.where(key_pos <= query_pos, raw, masked_score), key_pos)


def stats_pass(queries, key_set, start):
    length = key_set.shape[0]
    blk = block_length()
    key_blocks = key_set.reshape(length // blk, blk, key_set.shape[1])
    heads_here, window = (queries.shape[0], queries.shape[1])

    def stats_advance(running, element):
        row_max, row_sum = running
        block_index, key_block = element
        scores, key_pos = scores_of(queries, key_block, start + block_index * blk)
        new_max = jnp.maximum(row_max, jnp.max(scores, axis=-1))
        row_sum = row_sum * jnp.exp(row_max - new_max) + jnp.sum(
            jnp.exp(scores - new_max[..., None]), axis=-1
        )
        return ((new_max, row_sum), None)

    initial = (
        jnp.full((heads_here, window), masked_score, jnp.float32),
        jnp.zeros((heads_here, window), jnp.float32),
    )
    (row_max, row_sum), unused = lax.scan(
        stats_advance, initial, (jnp.arange(length // blk, dtype=jnp.int32), key_blocks)
    )
    return (row_max, row_sum)


def weight_pass(queries, key_set, value_set, start, row_max, row_sum):
    length = key_set.shape[0]
    blk = block_length()
    key_blocks = key_set.reshape(length // blk, blk, key_set.shape[1])
    value_blocks = value_set.reshape(length // blk, blk, value_set.shape[1])
    prefix = SEQ - queries.shape[1]

    def weight_advance(partial_value, element):
        block_index, key_block, value_block = element
        scores, key_pos = scores_of(queries, key_block, start + block_index * blk)
        weights = jnp.exp(scores - row_max[..., None]) / row_sum[..., None]
        vote_sum = jnp.sum(jnp.where(key_pos < prefix, weights, 0.0), axis=(0, 1))
        partial_value = partial_value + jnp.einsum(
            "hwp,pd->hwd",
            weights.astype(jnp.bfloat16),
            value_block,
            preferred_element_type=jnp.float32,
        )
        return (partial_value, vote_sum)

    initial = jnp.zeros((queries.shape[0], queries.shape[1], value_set.shape[1]), jnp.float32)
    partial_value, vote_sum = lax.scan(
        weight_advance,
        initial,
        (jnp.arange(length // blk, dtype=jnp.int32), key_blocks, value_blocks),
    )
    return (partial_value, vote_sum.reshape(length))


def pool_votes(padded, length):
    pooled = padded[0:length]
    for offset in range(1, 7):
        pooled = pooled + padded[offset : offset + length]
    return pooled * ((SEQ - WIN) / (7.0 * (HQ // KVH) * WIN))


def on_device(window_queries, key_rows, value_rows, kept):
    row_count = key_rows.shape[0]
    half_len = key_rows.shape[1]
    head_dim = key_rows.shape[2]
    window = window_queries.shape[0]
    owners = lax.axis_size("tp")
    device = lax.axis_index("tp")
    local_heads = window_queries.shape[1] // head_dim
    queries = window_queries.reshape(window, local_heads, head_dim).transpose(1, 0, 2)
    no_rim = jnp.zeros((3,), jnp.float32)
    side = device % 2
    is_first = side == 0
    partner_q = partner(queries, "tp", 0)
    group_q = lax.cond(
        is_first,
        lambda: jnp.concatenate([queries, partner_q]),
        lambda: jnp.concatenate([partner_q, queries]),
    )
    start = side * half_len
    row_max, row_sum = stats_pass(group_q, key_rows[0], start)
    other_max, other_sum = partner((row_max, row_sum), "tp", 0)
    both_max = jnp.maximum(row_max, other_max)
    both_sum = row_sum * jnp.exp(row_max - both_max) + other_sum * jnp.exp(other_max - both_max)
    partial_value, vote_sum = weight_pass(
        group_q, key_rows[0], value_rows[0], start, both_max, both_sum
    )
    own_part = lax.dynamic_slice_in_dim(partial_value, side * local_heads, local_heads, 0)
    their_part = lax.dynamic_slice_in_dim(partial_value, (1 - side) * local_heads, local_heads, 0)
    out_heads = own_part + partner(their_part, "tp", 0)
    rim_send = jnp.concatenate([vote_sum[:3], vote_sum[-3:]])
    rim_got = partner(rim_send, "tp", 0)
    left_rim = jnp.where(is_first, no_rim, rim_got[3:])
    right_rim = jnp.where(is_first, rim_got[:3], no_rim)
    pooled_rows = pool_votes(jnp.concatenate([left_rim, vote_sum, right_rim]), half_len)[None]
    window_out = (
        out_heads.transpose(1, 0, 2).reshape(window, local_heads * head_dim).astype(jnp.bfloat16)
    )
    per_half = kept.shape[1] // 2
    capacity = 2 * per_half // owners
    global_row = device * row_count + 0
    head_index = global_row // 2
    side_of = global_row % 2
    positions = lax.dynamic_slice(kept, (head_index, side_of * per_half), (1, per_half))[0]
    local_pos = positions - side_of * half_len
    owner_of = positions // OWNER_BLOCK % owners
    one_hot = (owner_of[:, None] == jnp.arange(owners, dtype=jnp.int32)[None, :]).astype(jnp.int32)
    rank_of = jnp.sum(jnp.cumsum(one_hot, axis=0) * one_hot, axis=1) - 1
    slot_of = owner_of * capacity + rank_of
    source_row = jnp.zeros((owners * capacity,), jnp.int32).at[slot_of].set(local_pos)
    occupied = jnp.zeros((owners * capacity,), jnp.int32).at[slot_of].set(1) == 1
    key_pick = jnp.where(occupied[:, None], key_rows[0][source_row], 0)
    value_pick = jnp.where(occupied[:, None], value_rows[0][source_row], 0)
    vote_pick = jnp.where(occupied, pooled_rows[0][source_row], 0.0).astype(jnp.bfloat16)
    key_send = [key_pick.reshape(owners, capacity, head_dim)]
    value_send = [value_pick.reshape(owners, capacity, head_dim)]
    vote_send = [vote_pick.reshape(owners, capacity)]
    key_buffer = jnp.stack(key_send, axis=1)
    value_buffer = jnp.stack(value_send, axis=1)
    vote_buffer = jnp.stack(vote_send, axis=1)
    got_keys, got_values, got_votes = in_one_piece(
        (key_buffer, value_buffer, vote_buffer), "tp", 0, 1, 3
    )
    kept_keys = got_keys.reshape(1, KVH, 2 * capacity, head_dim)
    kept_values = got_values.reshape(1, KVH, 2 * capacity, head_dim)
    kept_votes = got_votes.reshape(1, KVH, 2 * capacity)
    return (window_out, kept_keys, kept_values, kept_votes)


def solution(mesh):
    return jax.shard_map(
        on_device,
        mesh=mesh,
        in_specs=(P("grp", "tp"), P("tp", "grp", None), P("tp", "grp", None), P(None, "grp")),
        out_specs=(
            P("grp", "tp"),
            P("tp", None, "grp", None),
            P("tp", None, "grp", None),
            P("tp", "grp", None),
        ),
        check_vma=False,
    )
```

profile of v0, /device:TPU:224, one launch (start us, length us, event | category | flops | bytes accessed | tf_op | source)
XLA Modules:
  0.0 165.9 jit_solution(16925565986795675145)
XLA Ops:
  0.6 0.9 copy.44
  1.5 1.6 collective-permute-start
  3.1 0.8 dynamic_slice.28
  3.9 4.5 %reduce-window.6 = s32[16,8,128]{2,1,0:T(8,128)S(1)} reduce-window(s32[16,8,128]{2,1,0:T(8,128)S(1)} %fusion.34, s32[]{:T(128)} %constant.115.clone.1), window={size=1x1x128 pad=0_0x0_0x127_0}, to_apply=%region_9.10 | reduce-window | flops 2080768 | bytes 131076 | tf_op jit(solution)/shard_map/reduce-window
  8.9 0.9 compare_select_fusion
  9.8 4.3 %scatter_custom_fusion.1 = s32[2048]{0:T(1024)S(1)} fusion(s32[1024]{0:T(1024)S(1)} %bitcast.138, s32[1024]{0:T(1024)S(1)} %get-tuple-element.229, s32[]{:T(128)} %constant.115.clone.1), kind=kCustom, calls=%fused_computation.111 | custom fusion | bytes 8196 | tf_op jit(solution)/shard_map/scatter | solution.py:157
  14.3 34.9 %while.26 = (s32[]{:T(128)}, f32[16,32]{1,0:T(8,128)S(1)}, f32[16,32]{1,0:T(8,128)S(1)}, s32[8]{0:T(128)S(1)}, s32[]{:T(128)}, /*index=5*/bf16[8,2048,128]{2,1,0...) while((s32[]{:T(128)}, f32[16,32]{1,0:T(8,128)S(1)}, ...), condition=%wide.region_5.6_spmd.clone, body=%wide.region_2.5_spmd.clone.sunk | while | flops 275845664 | bytes 9284004 | solution.py:67
  14.3 0.6 dynamic_slice.62
  15.7 1.9 %fusion.64 = (f32[16,32]{1,0:T(8,128)S(1)}, f32[2048,16,32]{0,2,1:T(8,128)S(1)}) fusion(pred[32,2048]{1,0:T(8,128)(4,1)S(1)} %broadcast_compare_fusion.8, bf16[16,32,128]{2,1,0:T(8,128)(2,1)S(1)} %get-tuple-element.375, bf16[8,2048,128]{2,1,0:T(8,128)(2,1)} %get-tuple-element.374, s32[]{:T(128)S(6)} %copy.55), kind=kOutput, calls=%fused_computation.9.clone.1 | convolution fusion | flops 271580672 | bytes 4917252 | tf_op jit(solution)/shard_map/while/body/eval_jaxpr/hwd,pd->hwp/dot_general | solution.py:40
  17.6 1.0 exponential_reduce_fusion.2
  18.6 0.6 dynamic_slice.62
  20.0 1.9 %fusion.64 = (f32[16,32]{1,0:T(8,128)S(1)}, f32[2048,16,32]{0,2,1:T(8,128)S(1)}) fusion(pred[32,2048]{1,0:T(8,128)(4,1)S(1)} %broadcast_compare_fusion.8, bf16[16,32,128]{2,1,0:T(8,128)(2,1)S(1)} %get-tuple-element.375, bf16[8,2048,128]{2,1,0:T(8,128)(2,1)} %get-tuple-element.374, s32[]{:T(128)S(6)} %copy.55), kind=kOutput, calls=%fused_computation.9.clone.1 | convolution fusion | flops 271580672 | bytes 4917252 | tf_op jit(solution)/shard_map/while/body/eval_jaxpr/hwd,pd->hwp/dot_general | solution.py:40
  21.9 1.0 exponential_reduce_fusion.2
  23.0 0.6 dynamic_slice.62
  24.4 1.9 %fusion.64 = (f32[16,32]{1,0:T(8,128)S(1)}, f32[2048,16,32]{0,2,1:T(8,128)S(1)}) fusion(pred[32,2048]{1,0:T(8,128)(4,1)S(1)} %broadcast_compare_fusion.8, bf16[16,32,128]{2,1,0:T(8,128)(2,1)S(1)} %get-tuple-element.375, bf16[8,2048,128]{2,1,0:T(8,128)(2,1)} %get-tuple-element.374, s32[]{:T(128)S(6)} %copy.55), kind=kOutput, calls=%fused_computation.9.clone.1 | convolution fusion | flops 271580672 | bytes 4917252 | tf_op jit(solution)/shard_map/while/body/eval_jaxpr/hwd,pd->hwp/dot_general | solution.py:40
  26.3 1.0 exponential_reduce_fusion.2
  27.4 0.6 dynamic_slice.62
  28.7 1.9 %fusion.64 = (f32[16,32]{1,0:T(8,128)S(1)}, f32[2048,16,32]{0,2,1:T(8,128)S(1)}) fusion(pred[32,2048]{1,0:T(8,128)(4,1)S(1)} %broadcast_compare_fusion.8, bf16[16,32,128]{2,1,0:T(8,128)(2,1)S(1)} %get-tuple-element.375, bf16[8,2048,128]{2,1,0:T(8,128)(2,1)} %get-tuple-element.374, s32[]{:T(128)S(6)} %copy.55), kind=kOutput, calls=%fused_computation.9.clone.1 | convolution fusion | flops 271580672 | bytes 4917252 | tf_op jit(solution)/shard_map/while/body/eval_jaxpr/hwd,pd->hwp/dot_general | solution.py:40
  30.7 1.0 exponential_reduce_fusion.2
  31.7 0.6 dynamic_slice.62
  33.1 1.9 %fusion.64 = (f32[16,32]{1,0:T(8,128)S(1)}, f32[2048,16,32]{0,2,1:T(8,128)S(1)}) fusion(pred[32,2048]{1,0:T(8,128)(4,1)S(1)} %broadcast_compare_fusion.8, bf16[16,32,128]{2,1,0:T(8,128)(2,1)S(1)} %get-tuple-element.375, bf16[8,2048,128]{2,1,0:T(8,128)(2,1)} %get-tuple-element.374, s32[]{:T(128)S(6)} %copy.55), kind=kOutput, calls=%fused_computation.9.clone.1 | convolution fusion | flops 271580672 | bytes 4917252 | tf_op jit(solution)/shard_map/while/body/eval_jaxpr/hwd,pd->hwp/dot_general | solution.py:40
  35.0 1.0 exponential_reduce_fusion.2
  36.1 0.6 dynamic_slice.62
  37.5 1.9 %fusion.64 = (f32[16,32]{1,0:T(8,128)S(1)}, f32[2048,16,32]{0,2,1:T(8,128)S(1)}) fusion(pred[32,2048]{1,0:T(8,128)(4,1)S(1)} %broadcast_compare_fusion.8, bf16[16,32,128]{2,1,0:T(8,128)(2,1)S(1)} %get-tuple-element.375, bf16[8,2048,128]{2,1,0:T(8,128)(2,1)} %get-tuple-element.374, s32[]{:T(128)S(6)} %copy.55), kind=kOutput, calls=%fused_computation.9.clone.1 | convolution fusion | flops 271580672 | bytes 4917252 | tf_op jit(solution)/shard_map/while/body/eval_jaxpr/hwd,pd->hwp/dot_general | solution.py:40
  39.4 1.0 exponential_reduce_fusion.2
  41.8 1.9 %fusion.64 = (f32[16,32]{1,0:T(8,128)S(1)}, f32[2048,16,32]{0,2,1:T(8,128)S(1)}) fusion(pred[32,2048]{1,0:T(8,128)(4,1)S(1)} %broadcast_compare_fusion.8, bf16[16,32,128]{2,1,0:T(8,128)(2,1)S(1)} %get-tuple-element.375, bf16[8,2048,128]{2,1,0:T(8,128)(2,1)} %get-tuple-element.374, s32[]{:T(128)S(6)} %copy.55), kind=kOutput, calls=%fused_computation.9.clone.1 | convolution fusion | flops 271580672 | bytes 4917252 | tf_op jit(solution)/shard_map/while/body/eval_jaxpr/hwd,pd->hwp/dot_general | solution.py:40
  43.7 1.0 exponential_reduce_fusion.2
  44.8 0.6 dynamic_slice.62
  46.2 1.9 %fusion.64 = (f32[16,32]{1,0:T(8,128)S(1)}, f32[2048,16,32]{0,2,1:T(8,128)S(1)}) fusion(pred[32,2048]{1,0:T(8,128)(4,1)S(1)} %broadcast_compare_fusion.8, bf16[16,32,128]{2,1,0:T(8,128)(2,1)S(1)} %get-tuple-element.375, bf16[8,2048,128]{2,1,0:T(8,128)(2,1)} %get-tuple-element.374, s32[]{:T(128)S(6)} %copy.55), kind=kOutput, calls=%fused_computation.9.clone.1 | convolution fusion | flops 271580672 | bytes 4917252 | tf_op jit(solution)/shard_map/while/body/eval_jaxpr/hwd,pd->hwp/dot_general | solution.py:40
  48.1 1.0 exponential_reduce_fusion.2
  49.2 0.6 collective-permute-start.2
  49.8 1.5 collective-permute-start.1
  51.3 4.3 %scatter_custom_fusion = s32[2048]{0:T(1024)S(1)} fusion(s32[1024]{0:T(1024)S(1)} %bitcast.139, s32[1024]{0:T(1024)S(1)} %ne.102, s32[]{:T(128)} %constant.115.clone.1), kind=kCustom, calls=%fused_computation.113 | custom fusion | bytes 8196 | tf_op jit(solution)/shard_map/scatter | solution.py:158
  55.6 8.3 %gather_fusion.1 = bf16[2048,128]{1,0:T(8,128)(2,1)S(1)} fusion(bf16[16384,128]{1,0:T(8,128)(2,1)} %bitcast.116, s32[2048]{0:T(1024)S(1)} %fusion.35), kind=kCustom, calls=%fused_computation.1 | custom fusion | bytes 1056768 | tf_op jit(solution)/shard_map/gather | solution.py:160
  64.2 8.3 %gather_fusion = bf16[2048,128]{1,0:T(8,128)(2,1)S(1)} fusion(bf16[16384,128]{1,0:T(8,128)(2,1)} %bitcast.115, s32[2048]{0:T(1024)S(1)} %fusion.35), kind=kCustom, calls=%fused_computation | custom fusion | bytes 1056768 | tf_op jit(solution)/shard_map/gather | solution.py:159
  72.9 48.2 %while.27 = (s32[]{:T(128)}, f32[16,32,128]{2,1,0:T(8,128)S(1)}, f32[8,2048]{1,0:T(8,128)S(1)}, s32[8]{0:T(128)S(1)}, s32[]{:T(128)}, /*index=5*/bf16[8,2048,128...) while((s32[]{:T(128)}, f32[16,32,128]{2,1,0:T(8,128)S(1)}, ...), condition=%wide.region_8.9_spmd.clone, body=%wide.region_6.8_spmd.clone.sunk | while | flops 544411648 | bytes 6078919 | solution.py:94
  72.9 0.6 dynamic_slice.65
  74.3 2.6 %select_reduce_fusion.2 = (f32[2048]{0:T(1024)S(1)}, bf16[16,32,2048]{2,1,0:T(8,128)(2,1)S(1)}) fusion(pred[2048]{0:T(1024)(128)(4,1)S(1)} %broadcast_compare_fusion.9, f32[16,32]{1,0:T(8,128)S(1)} %get-tuple-element.413, f32[16,32]{1,0:T(8,128)S(1)} %get-tuple-element.412, bf16[16,32,128]{2,1,0:T(8,128)(2,1)S(1)} %get-tuple-element.411, ...), kind=kOutput, calls=%fused_computation.24.clone.1 | convolution fusion | flops 275773440 | bytes 2832388 | tf_op jit(solution)/shard_map/while/body/eval_jaxpr/hwd,pd->hwp/dot_general | solution.py:40
  76.9 1.8 %fusion.69 = f32[16,32,128]{2,1,0:T(8,128)S(1)} fusion(bf16[16,32,2048]{2,1,0:T(8,128)(2,1)S(1)} %get-tuple-element.347, bf16[8,2048,128]{2,1,0:T(8,128)(2,1)} %get-tuple-element.414, s32[]{:T(128)S(6)} %copy.64, f32[16,32,128]{2,1,0:T(8,128)S(1)} %get-tuple-element.393, pred[]{:T(512)S(6)} %compare.35), kind=kOutput, calls=%fused_computation.27.clone.1 | convolution fusion | flops 268566528 | bytes 3145733 | tf_op jit(solution)/shard_map/while/body/eval_jaxpr/hwp,pd->hwd/dot_general | solution.py:85
  80.3 2.6 %select_reduce_fusion.2 = (f32[2048]{0:T(1024)S(1)}, bf16[16,32,2048]{2,1,0:T(8,128)(2,1)S(1)}) fusion(pred[2048]{0:T(1024)(128)(4,1)S(1)} %broadcast_compare_fusion.9, f32[16,32]{1,0:T(8,128)S(1)} %get-tuple-element.413, f32[16,32]{1,0:T(8,128)S(1)} %get-tuple-element.412, bf16[16,32,128]{2,1,0:T(8,128)(2,1)S(1)} %get-tuple-element.411, ...), kind=kOutput, calls=%fused_computation.24.clone.1 | convolution fusion | flops 275773440 | bytes 2832388 | tf_op jit(solution)/shard_map/while/body/eval_jaxpr/hwd,pd->hwp/dot_general | solution.py:40
  82.9 1.8 %fusion.69 = f32[16,32,128]{2,1,0:T(8,128)S(1)} fusion(bf16[16,32,2048]{2,1,0:T(8,128)(2,1)S(1)} %get-tuple-element.347, bf16[8,2048,128]{2,1,0:T(8,128)(2,1)} %get-tuple-element.414, s32[]{:T(128)S(6)} %copy.64, f32[16,32,128]{2,1,0:T(8,128)S(1)} %get-tuple-element.393, pred[]{:T(512)S(6)} %compare.35), kind=kOutput, calls=%fused_computation.27.clone.1 | convolution fusion | flops 268566528 | bytes 3145733 | tf_op jit(solution)/shard_map/while/body/eval_jaxpr/hwp,pd->hwd/dot_general | solution.py:85
  86.4 2.6 %select_reduce_fusion.2 = (f32[2048]{0:T(1024)S(1)}, bf16[16,32,2048]{2,1,0:T(8,128)(2,1)S(1)}) fusion(pred[2048]{0:T(1024)(128)(4,1)S(1)} %broadcast_compare_fusion.9, f32[16,32]{1,0:T(8,128)S(1)} %get-tuple-element.413, f32[16,32]{1,0:T(8,128)S(1)} %get-tuple-element.412, bf16[16,32,128]{2,1,0:T(8,128)(2,1)S(1)} %get-tuple-element.411, ...), kind=kOutput, calls=%fused_computation.24.clone.1 | convolution fusion | flops 275773440 | bytes 2832388 | tf_op jit(solution)/shard_map/while/body/eval_jaxpr/hwd,pd->hwp/dot_general | solution.py:40
  89.0 1.8 %fusion.69 = f32[16,32,128]{2,1,0:T(8,128)S(1)} fusion(bf16[16,32,2048]{2,1,0:T(8,128)(2,1)S(1)} %get-tuple-element.347, bf16[8,2048,128]{2,1,0:T(8,128)(2,1)} %get-tuple-element.414, s32[]{:T(128)S(6)} %copy.64, f32[16,32,128]{2,1,0:T(8,128)S(1)} %get-tuple-element.393, pred[]{:T(512)S(6)} %compare.35), kind=kOutput, calls=%fused_computation.27.clone.1 | convolution fusion | flops 268566528 | bytes 3145733 | tf_op jit(solution)/shard_map/while/body/eval_jaxpr/hwp,pd->hwd/dot_general | solution.py:85
  92.4 2.6 %select_reduce_fusion.2 = (f32[2048]{0:T(1024)S(1)}, bf16[16,32,2048]{2,1,0:T(8,128)(2,1)S(1)}) fusion(pred[2048]{0:T(1024)(128)(4,1)S(1)} %broadcast_compare_fusion.9, f32[16,32]{1,0:T(8,128)S(1)} %get-tuple-element.413, f32[16,32]{1,0:T(8,128)S(1)} %get-tuple-element.412, bf16[16,32,128]{2,1,0:T(8,128)(2,1)S(1)} %get-tuple-element.411, ...), kind=kOutput, calls=%fused_computation.24.clone.1 | convolution fusion | flops 275773440 | bytes 2832388 | tf_op jit(solution)/shard_map/while/body/eval_jaxpr/hwd,pd->hwp/dot_general | solution.py:40
  95.0 1.8 %fusion.69 = f32[16,32,128]{2,1,0:T(8,128)S(1)} fusion(bf16[16,32,2048]{2,1,0:T(8,128)(2,1)S(1)} %get-tuple-element.347, bf16[8,2048,128]{2,1,0:T(8,128)(2,1)} %get-tuple-element.414, s32[]{:T(128)S(6)} %copy.64, f32[16,32,128]{2,1,0:T(8,128)S(1)} %get-tuple-element.393, pred[]{:T(512)S(6)} %compare.35), kind=kOutput, calls=%fused_computation.27.clone.1 | convolution fusion | flops 268566528 | bytes 3145733 | tf_op jit(solution)/shard_map/while/body/eval_jaxpr/hwp,pd->hwd/dot_general | solution.py:85
  98.4 2.6 %select_reduce_fusion.2 = (f32[2048]{0:T(1024)S(1)}, bf16[16,32,2048]{2,1,0:T(8,128)(2,1)S(1)}) fusion(pred[2048]{0:T(1024)(128)(4,1)S(1)} %broadcast_compare_fusion.9, f32[16,32]{1,0:T(8,128)S(1)} %get-tuple-element.413, f32[16,32]{1,0:T(8,128)S(1)} %get-tuple-element.412, bf16[16,32,128]{2,1,0:T(8,128)(2,1)S(1)} %get-tuple-element.411, ...), kind=kOutput, calls=%fused_computation.24.clone.1 | convolution fusion | flops 275773440 | bytes 2832388 | tf_op jit(solution)/shard_map/while/body/eval_jaxpr/hwd,pd->hwp/dot_general | solution.py:40
  101.0 1.8 %fusion.69 = f32[16,32,128]{2,1,0:T(8,128)S(1)} fusion(bf16[16,32,2048]{2,1,0:T(8,128)(2,1)S(1)} %get-tuple-element.347, bf16[8,2048,128]{2,1,0:T(8,128)(2,1)} %get-tuple-element.414, s32[]{:T(128)S(6)} %copy.64, f32[16,32,128]{2,1,0:T(8,128)S(1)} %get-tuple-element.393, pred[]{:T(512)S(6)} %compare.35), kind=kOutput, calls=%fused_computation.27.clone.1 | convolution fusion | flops 268566528 | bytes 3145733 | tf_op jit(solution)/shard_map/while/body/eval_jaxpr/hwp,pd->hwd/dot_general | solution.py:85
  104.4 2.6 %select_reduce_fusion.2 = (f32[2048]{0:T(1024)S(1)}, bf16[16,32,2048]{2,1,0:T(8,128)(2,1)S(1)}) fusion(pred[2048]{0:T(1024)(128)(4,1)S(1)} %broadcast_compare_fusion.9, f32[16,32]{1,0:T(8,128)S(1)} %get-tuple-element.413, f32[16,32]{1,0:T(8,128)S(1)} %get-tuple-element.412, bf16[16,32,128]{2,1,0:T(8,128)(2,1)S(1)} %get-tuple-element.411, ...), kind=kOutput, calls=%fused_computation.24.clone.1 | convolution fusion | flops 275773440 | bytes 2832388 | tf_op jit(solution)/shard_map/while/body/eval_jaxpr/hwd,pd->hwp/dot_general | solution.py:40
  107.0 1.8 %fusion.69 = f32[16,32,128]{2,1,0:T(8,128)S(1)} fusion(bf16[16,32,2048]{2,1,0:T(8,128)(2,1)S(1)} %get-tuple-element.347, bf16[8,2048,128]{2,1,0:T(8,128)(2,1)} %get-tuple-element.414, s32[]{:T(128)S(6)} %copy.64, f32[16,32,128]{2,1,0:T(8,128)S(1)} %get-tuple-element.393, pred[]{:T(512)S(6)} %compare.35), kind=kOutput, calls=%fused_computation.27.clone.1 | convolution fusion | flops 268566528 | bytes 3145733 | tf_op jit(solution)/shard_map/while/body/eval_jaxpr/hwp,pd->hwd/dot_general | solution.py:85
  110.4 2.6 %select_reduce_fusion.2 = (f32[2048]{0:T(1024)S(1)}, bf16[16,32,2048]{2,1,0:T(8,128)(2,1)S(1)}) fusion(pred[2048]{0:T(1024)(128)(4,1)S(1)} %broadcast_compare_fusion.9, f32[16,32]{1,0:T(8,128)S(1)} %get-tuple-element.413, f32[16,32]{1,0:T(8,128)S(1)} %get-tuple-element.412, bf16[16,32,128]{2,1,0:T(8,128)(2,1)S(1)} %get-tuple-element.411, ...), kind=kOutput, calls=%fused_computation.24.clone.1 | convolution fusion | flops 275773440 | bytes 2832388 | tf_op jit(solution)/shard_map/while/body/eval_jaxpr/hwd,pd->hwp/dot_general | solution.py:40
  113.0 1.8 %fusion.69 = f32[16,32,128]{2,1,0:T(8,128)S(1)} fusion(bf16[16,32,2048]{2,1,0:T(8,128)(2,1)S(1)} %get-tuple-element.347, bf16[8,2048,128]{2,1,0:T(8,128)(2,1)} %get-tuple-element.414, s32[]{:T(128)S(6)} %copy.64, f32[16,32,128]{2,1,0:T(8,128)S(1)} %get-tuple-element.393, pred[]{:T(512)S(6)} %compare.35), kind=kOutput, calls=%fused_computation.27.clone.1 | convolution fusion | flops 268566528 | bytes 3145733 | tf_op jit(solution)/shard_map/while/body/eval_jaxpr/hwp,pd->hwd/dot_general | solution.py:85
  116.5 2.6 %select_reduce_fusion.2 = (f32[2048]{0:T(1024)S(1)}, bf16[16,32,2048]{2,1,0:T(8,128)(2,1)S(1)}) fusion(pred[2048]{0:T(1024)(128)(4,1)S(1)} %broadcast_compare_fusion.9, f32[16,32]{1,0:T(8,128)S(1)} %get-tuple-element.413, f32[16,32]{1,0:T(8,128)S(1)} %get-tuple-element.412, bf16[16,32,128]{2,1,0:T(8,128)(2,1)S(1)} %get-tuple-element.411, ...), kind=kOutput, calls=%fused_computation.24.clone.1 | convolution fusion | flops 275773440 | bytes 2832388 | tf_op jit(solution)/shard_map/while/body/eval_jaxpr/hwd,pd->hwp/dot_general | solution.py:40
  119.1 1.8 %fusion.69 = f32[16,32,128]{2,1,0:T(8,128)S(1)} fusion(bf16[16,32,2048]{2,1,0:T(8,128)(2,1)S(1)} %get-tuple-element.347, bf16[8,2048,128]{2,1,0:T(8,128)(2,1)} %get-tuple-element.414, s32[]{:T(128)S(6)} %copy.64, f32[16,32,128]{2,1,0:T(8,128)S(1)} %get-tuple-element.393, pred[]{:T(512)S(6)} %compare.35), kind=kOutput, calls=%fused_computation.27.clone.1 | convolution fusion | flops 268566528 | bytes 3145733 | tf_op jit(solution)/shard_map/while/body/eval_jaxpr/hwp,pd->hwd/dot_general | solution.py:85
  121.8 3.1 %collective-permute-done.4 = f32[6]{0:T(128)S(1)} collective-permute-done((f32[6]{0:T(128)S(1)}, f32[6]{0:T(128)S(1)}, u32[]{:S(2)}, u32[]{:S(2)}) %collective-permute-start.4) | collective-permute-done | bytes 56 | tf_op jit(solution)/shard_map/ppermute | solution.py:21
  125.1 13.1 %gather_fusion.2 = bf16[2048]{0:T(1024)(128)(2,1)S(1)} fusion(bf16[16384]{0:T(1024)(128)(2,1)S(1)} %fusion.23, s32[2048]{0:T(1024)S(1)} %fusion.35), kind=kCustom, calls=%fused_computation.2 | custom fusion | bytes 16384 | tf_op jit(solution)/shard_map/gather | solution.py:161
  138.3 1.1 pad_maximum_fusion.2
  139.4 6.7 %all-to-all-start = ((bf16[16,1,128,257]{2,3,1,0:T(8,128)(2,1)}), bf16[16,1,128,257]{2,3,1,0:T(8,128)(2,1)S(1)}, u32[]{:S(2)}, u32[]{:S(2)}) async-start(bf16[16,1,128,257]{2,3,1,0:T(8,128)(2,1)} %pad_maximum_fusion.2), calls=%async_computation | async-start | bytes 2162688 | tf_op jit(solution)/shard_map/all_to_all | solution.py:29
  146.1 2.0 %collective-permute-start.3 = (f32[8,32,128]{2,1,0:T(8,128)S(1)}, f32[8,32,128]{2,1,0:T(8,128)S(1)}, u32[]{:S(2)}, u32[]{:S(2)}) collective-permute-start(f32[8,32,128]{2,1,0:T(8,128)S(1)} %constant_dynamic-slice_fusion), channel_id=1, source_target_pairs={{0,1},{1,0},{2,3},{3,2},{4,5},{5,4},{6,7},{7,6},{8,9},{9,8},{10,11... | collective-permute-start | bytes 393224 | tf_op jit(solution)/shard_map/ppermute | solution.py:21
  148.1 12.8 %collective-permute-done.3 = f32[8,32,128]{2,1,0:T(8,128)S(1)} collective-permute-done((f32[8,32,128]{2,1,0:T(8,128)S(1)}, f32[8,32,128]{2,1,0:T(8,128)S(1)}, u32[]{:S(2)}, u32[]{:S(2)}) %collective-permute-start.3) | collective-permute-done | bytes 131104 | tf_op jit(solution)/shard_map/ppermute | solution.py:21
  160.9 0.6 copy_bitcast_fusion
  161.6 1.5 all-to-all-done
  163.0 0.8 copy.42
  164.1 1.3 fusion.50
  165.3 0.6 reshape_reshape.3
  (136 shorter events, 10.8 us)
Async XLA Ops:
  1.5 12.7 %collective-permute-start = (bf16[8,32,128]{2,0,1:T(8,128)(2,1)S(1)}, bf16[8,32,128]{2,0,1:T(8,128)(2,1)S(1)}, u32[]{:S(2)}, u32[]{:S(2)}) collective-permute-start(bf16[8,32,128]{2,0,1:T(8,128)(2,1)S(1)} %bitcast.122), channel_id=1, source_target_pairs={{0,1},{1,0},{2,3},{3,2},{4,5},{5,4},{6,7},{7,6},{8,9},{9,8},{10,11... | collective-permute-start | bytes 196616 | tf_op jit(solution)/shard_map/ppermute | solution.py:21
  49.2 23.7 %collective-permute-start.2 = (f32[16,32]{1,0:T(8,128)S(1)}, f32[16,32]{1,0:T(8,128)S(1)}, u32[]{:S(2)}, u32[]{:S(2)}) collective-permute-start(f32[16,32]{1,0:T(8,128)S(1)} %get-tuple-element.111), channel_id=1, source_target_pairs={{0,1},{1,0},{2,3},{3,2},{4,5},{5,4},{6,7},{7,6},{8,9},{9,8},{10,11... | collective-permute-start | bytes 6152 | tf_op jit(solution)/shard_map/ppermute | solution.py:21
  49.8 23.1 %collective-permute-start.1 = (f32[16,32]{1,0:T(8,128)S(1)}, f32[16,32]{1,0:T(8,128)S(1)}, u32[]{:S(2)}, u32[]{:S(2)}) collective-permute-start(f32[16,32]{1,0:T(8,128)S(1)} %get-tuple-element.110), channel_id=1, source_target_pairs={{0,1},{1,0},{2,3},{3,2},{4,5},{5,4},{6,7},{7,6},{8,9},{9,8},{10,11... | collective-permute-start | bytes 6152 | tf_op jit(solution)/shard_map/ppermute | solution.py:21
  121.3 3.6 %collective-permute-start.4 = (f32[6]{0:T(128)S(1)}, f32[6]{0:T(128)S(1)}, u32[]{:S(2)}, u32[]{:S(2)}) collective-permute-start(f32[6]{0:T(128)S(1)} %pad_maximum_fusion.5), channel_id=1, source_target_pairs={{0,1},{1,0},{2,3},{3,2},{4,5},{5,4},{6,7},{7,6},{8,9},{9,8},{10,11... | collective-permute-start | bytes 80 | tf_op jit(solution)/shard_map/ppermute | solution.py:21
  139.4 23.7 %all-to-all-start = ((bf16[16,1,128,257]{2,3,1,0:T(8,128)(2,1)}), bf16[16,1,128,257]{2,3,1,0:T(8,128)(2,1)S(1)}, u32[]{:S(2)}, u32[]{:S(2)}) async-start(bf16[16,1,128,257]{2,3,1,0:T(8,128)(2,1)} %pad_maximum_fusion.2), calls=%async_computation | async-start | bytes 2162688 | tf_op jit(solution)/shard_map/all_to_all | solution.py:29
  146.1 14.8 %collective-permute-start.3 = (f32[8,32,128]{2,1,0:T(8,128)S(1)}, f32[8,32,128]{2,1,0:T(8,128)S(1)}, u32[]{:S(2)}, u32[]{:S(2)}) collective-permute-start(f32[8,32,128]{2,1,0:T(8,128)S(1)} %constant_dynamic-slice_fusion), channel_id=1, source_target_pairs={{0,1},{1,0},{2,3},{3,2},{4,5},{5,4},{6,7},{7,6},{8,9},{9,8},{10,11... | collective-permute-start | bytes 393224 | tf_op jit(solution)/shard_map/ppermute | solution.py:21
where the time goes:
time: 168 us; the launch traced here: 166 us
  local copies, waits for them, and re-layouts  55 us (33%)
  matrix products  50.3 us (30%)
  other arithmetic  18 us (11%)
  waiting for transfers between devices  17.3 us (10%)
  starting transfers between devices  12.9 us (8%)
  loops' own time  11.5 us (7%)
    dot_general x16, matrix products, scores_of(): jnp.einsum('hwd,pd->hwp', queries, key_block, preferred_element_type=jnp....  35.9 us
    ppermute x5, waiting for transfers between devices, partner(): return lax.ppermute(value, axis, pairs)  15.9 us
    dot_general x8, matrix products, weight_advance(): jnp.einsum('hwp,pd->hwd', weights.astype(jnp.bfloat16), value_block, pref...  14.4 us
    gather x1, local copies, waits for them, and re-layouts, on_device(): pooled_rows[0][source_row]  13.1 us
    dynamic_slice x16, local copies, waits for them, and re-layouts, stats_pass(): lax.scan(stats_advance, initial, (jnp.arange(length // blk, dtype=jnp.int...  9.38 us
    gather x2, local copies, waits for them, and re-layouts, on_device(): key_pick = jnp.where(occupied[:, None], key_rows[0][source_row], 0)  8.6 us
    gather x2, local copies, waits for them, and re-layouts, on_device(): value_pick = jnp.where(occupied[:, None], value_rows[0][source_row], 0)  8.6 us
    reduce_sum x8, other arithmetic, stats_advance(): jnp.sum(jnp.exp(scores - new_max[..., None]), axis=-1)  8.23 us
  transfers between devices with their start and end apart: 6, of which 3 were waited for; matrix products, arithmetic and copies ran while one was open for 20% of the time, Pallas kernels for 0%

commit v1 on v0

v1 whole, which is shorter than its diff:
```python
import functools

import jax
import jax.numpy as jnp
from jax import lax
from jax.experimental import pallas as pl
from jax.experimental.pallas import tpu as pltpu
from jax.sharding import PartitionSpec as P

SEQ = 32768
WIN = 32
HALF = 16384
CHUNKS = 8
OWNERS = 16
BLOCK = 128
ROWS = 256
CHUNK = OWNERS * BLOCK
SCALE = 1.4426950408889634 / 128.0**0.5
FACTOR = (SEQ - WIN) / (7.0 * 16 * WIN)
MASKED = -1e30
F32 = jnp.float32
BF16 = jnp.bfloat16
MESH = pl.DeviceIdType.MESH


def contract_last(a, b):
    return lax.dot_general(a, b, (((1,), (1,)), ((), ())), preferred_element_type=F32)


def mm(a, b):
    return jnp.dot(a, b, preferred_element_type=F32)


def iota(shape, dim):
    return lax.broadcasted_iota(jnp.int32, shape, dim)


def as_bf16(condition):
    return jnp.where(condition, 1.0, 0.0).astype(BF16)


def kernel(
    q_ref, k_hbm, v_hbm, kept_ref,
    wout_ref, kk_ref, vv_ref, vout_ref,
    kv, vt, ebuf, s_a, s_b, q_t, oacc, orecv, mrun, st_send, st_recv,
    slot_of, in_block, band, slot_hot, sendbuf, khalo, vext, vsend, vrecv, vstage,
    load_k, load_v, own_sem, a2a_send, a2a_recv, q_sem, halo_sem, st_sem, o_sem, vote_send, vote_recv,
):
    me = lax.axis_index("tp")
    grp = lax.axis_index("grp")
    side = me % 2
    head = me // 2
    mate = me + 1 - 2 * side

    def peer(rel):
        return (me + rel) % OWNERS

    def remote(src, dst, send, recv, to):
        return pltpu.make_async_remote_copy(
            src_ref=src, dst_ref=dst, send_sem=send, recv_sem=recv, device_id=(grp, to), device_id_type=MESH
        )

    def k_load(k):
        return pltpu.make_async_copy(k_hbm.at[k], kv.at[:, k, :, pl.ds(0, 128)], load_k.at[k])

    def v_load(k):
        return pltpu.make_async_copy(v_hbm.at[k], kv.at[:, k, :, pl.ds(128, 128)], load_v.at[k])

    barrier = pltpu.get_barrier_semaphore()
    for rel in range(1, OWNERS):
        pl.semaphore_signal(barrier, inc=1, device_id=(grp, peer(rel)), device_id_type=MESH)
    for k in range(CHUNKS):
        k_load(k).start()
        v_load(k).start()

    queries = jnp.concatenate([q_ref[:, a * 128 : (a + 1) * 128] for a in range(8)], axis=0)
    q_t[0] = queries.astype(F32).T.astype(BF16)

    mine = jnp.sum(jnp.where(iota((8, 2048), 0) == head, kept_ref[...], 0), axis=0, keepdims=True)
    pos = jnp.where(side == 0, mine[:, :1024], mine[:, 1024:] - HALF)
    blk = pos // BLOCK
    lane = pos % BLOCK
    hot_block = as_bf16(iota((128, 1024), 0) == blk)
    hot_lane = as_bf16(iota((128, 1024), 0) == lane)
    in_block[...] = hot_block
    away = iota((384, 1024), 0) - 128 - lane
    band[...] = as_bf16((away <= 3) & (away >= -3))
    mask = contract_last(hot_block, hot_lane)
    mask16 = mask.astype(BF16)
    r, c = iota((128, 128), 0), iota((128, 128), 1)
    before = mm(mask16, as_bf16(r < c))
    same = mm(as_bf16((c < r) & ((r - c) % OWNERS == 0)), mask16).astype(BF16)
    ahead = mm(same, jnp.ones((128, 128), BF16))
    slots = jnp.where(mask > 0.5, before + ahead, -1.0)
    slot_of[...] = slots
    picked = mm(slots.astype(BF16), hot_lane)
    slot_i = jnp.sum(jnp.where(hot_block > 0.5, picked, 0.0), axis=0, keepdims=True)
    slot_hot[...] = as_bf16(iota((128, 1024), 0).astype(F32) == slot_i)

    window_of = iota((WIN, ROWS), 1) % WIN
    hidden_row = iota((WIN, ROWS), 0) > window_of
    oacc[...] = jnp.zeros_like(oacc)

    def scores(k, group, s_ref):
        keys = kv[:, k, :, 0:128].reshape(CHUNK, 128)
        s = mm(keys, q_t[group])
        hide = jnp.logical_and(hidden_row, jnp.logical_and(side == 1, k == CHUNKS - 1))
        last = jnp.where(hide, MASKED, s[CHUNK - WIN :])
        s_ref[0 : CHUNK - WIN, :] = s[: CHUNK - WIN]
        s_ref[CHUNK - WIN :, :] = last
        return jnp.maximum(
            jnp.max(s[: CHUNK - WIN], axis=0, keepdims=True), jnp.max(last, axis=0, keepdims=True)
        )

    def transpose_values(k):
        for o in range(OWNERS):
            vt[k, 0:128, o * 128 : (o + 1) * 128] = kv[o, k, :, 128:256].T
        vt[k, 128:144, :] = jnp.ones((16, CHUNK), BF16)

    def weigh(k, group, s_ref, old, new):
        u = group * CHUNKS + k
        shift = new * SCALE
        e = jnp.exp2(s_ref[...] * SCALE - shift).astype(BF16)
        ebuf[u] = e
        alpha = jnp.exp2(old * SCALE - shift)
        mrun[u] = jnp.broadcast_to(new, (8, ROWS))
        oacc[group] = oacc[group] * alpha + mm(vt[k], e)

    def attend(group):
        def ready(k):
            if group == 0:
                k_load(k).wait()
                v_load(k).wait()

        def step(t, carry):
            m_old, mx = carry
            k0, k1 = 2 * t, 2 * t + 1
            ready(k1)
            if group == 0:
                transpose_values(k0)
                transpose_values(k1)
            m_new = jnp.maximum(m_old, mx)
            mx1 = scores(k1, group, s_b)
            weigh(k0, group, s_a, m_old, m_new)
            m_last = jnp.maximum(m_new, mx1)
            if group == 0:
                @pl.when(t < CHUNKS // 2 - 1)
                def _():
                    ready(k0 + 2)
            k2 = jnp.minimum(k0 + 2, CHUNKS - 1)
            mx2 = scores(k2, group, s_a)
            weigh(k1, group, s_b, m_new, m_last)
            return m_last, mx2

        ready(0)
        mx = scores(0, group, s_a)
        m, unused = lax.fori_loop(0, CHUNKS // 2, step, (jnp.full((1, ROWS), MASKED, F32), mx))
        st_send[group, 0:8, :] = jnp.broadcast_to(m, (8, ROWS))
        st_send[group, 8:16, :] = oacc[group, 128:136, :]
        return m

    m_own = attend(0)

    def pick(rel, unused):
        o = peer(rel)
        slot_row = iota((128, 128), 0).astype(F32)
        hot = jnp.concatenate(
            [as_bf16(slot_row == slot_of[pl.ds(16 * k + o, 1), :]) for k in range(CHUNKS)], axis=1
        )
        rows = mm(hot, kv[o].reshape(CHUNKS * 128, 256)).astype(BF16)
        sendbuf[o, 0] = rows[:, 0:128]
        sendbuf[o, 1] = rows[:, 128:256]
        return unused

    lax.fori_loop(0, OWNERS, pick, 0)

    pl.semaphore_wait(barrier, OWNERS - 1)
    q_copy = remote(q_t.at[0], q_t.at[1], q_sem.at[0], q_sem.at[1], mate)
    q_copy.start()
    edge_owner = 15 - 15 * side
    edge_chunk = 7 - 7 * side
    halo_copy = remote(
        kv.at[edge_owner, edge_chunk, :, pl.ds(0, 128)], khalo, halo_sem.at[0], halo_sem.at[1], mate
    )
    halo_copy.start()
    own_stat = remote(st_send.at[0], st_recv.at[0], st_sem.at[0], st_sem.at[1], mate)
    own_stat.start()

    def row_copies(rel):
        o = peer(rel)
        return [
            remote(
                sendbuf.at[o, n],
                out.at[head, pl.ds(side * 128, 128), :],
                a2a_send.at[n, rel],
                a2a_recv.at[n, rel],
                o,
            )
            for n, out in enumerate((kk_ref, vv_ref))
        ]

    def local_copies():
        return [
            pltpu.make_async_copy(sendbuf.at[me, n], out.at[head, pl.ds(side * 128, 128), :], own_sem.at[n])
            for n, out in enumerate((kk_ref, vv_ref))
        ]

    for rel in range(1, OWNERS):
        for copy in row_copies(rel):
            copy.start()
    for copy in local_copies():
        copy.start()

    q_copy.wait()
    m_mate = attend(1)
    mate_stat = remote(st_send.at[1], st_recv.at[1], st_sem.at[2], st_sem.at[3], mate)
    mate_stat.start()
    out_copy = remote(oacc.at[1], orecv, o_sem.at[0], o_sem.at[1], mate)
    out_copy.start()
    halo_copy.wait()
    s_halo = [mm(khalo[...], q_t[group]) for group in range(2)]
    own_stat.wait()
    mate_stat.wait()

    m_here = (m_own, m_mate)
    merged = []
    for group in range(2):
        m_there = st_recv[1 - group, 0:1, :]
        l_there = st_recv[1 - group, 8:9, :]
        m_all = jnp.maximum(m_here[group], m_there)
        here = jnp.exp2((m_here[group] - m_all) * SCALE)
        there = jnp.exp2((m_there - m_all) * SCALE)
        l_all = st_send[group, 8:9, :] * here + l_there * there
        merged.append((m_all, here, there, 1.0 / l_all))

    row_id = iota((16, ROWS), 0)

    def pieces(w):
        hi = w.astype(BF16).astype(F32)
        mid = (w - hi).astype(BF16).astype(F32)
        return jnp.where(row_id == 0, hi, jnp.where(row_id == 1, mid, 0.0)).astype(BF16)

    def tally(k, unused):
        total = jnp.zeros((16, CHUNK), F32)
        for group in range(2):
            m_all, here, there, inv = merged[group]
            u = group * CHUNKS + k
            w = jnp.exp2((mrun[u, 0:1, :] - m_all) * SCALE) * inv
            total = total + contract_last(pieces(w), ebuf[u])
        row = total[0:1, :] + total[1:2, :]
        for o in range(OWNERS):
            vext[pl.ds(8 + 16 * k + o, 1), :] = row[:, o * 128 : (o + 1) * 128]
        return unused

    lax.fori_loop(0, CHUNKS, tally, 0)
    halo_votes = jnp.zeros((16, 128), F32)
    for group in range(2):
        m_all, here, there, inv = merged[group]
        e = jnp.exp2(s_halo[group] * SCALE - m_all * SCALE).astype(BF16)
        halo_votes = halo_votes + contract_last(pieces(inv), e)
    halo_row = halo_votes[0:1, :] + halo_votes[1:2, :]
    vext[7:8, :] = jnp.where(side == 1, halo_row, 0.0)
    vext[136:137, :] = jnp.where(side == 0, halo_row, 0.0)
    cut = jnp.logical_and(iota((1, 128), 1) >= 128 - WIN, side == 1)
    vext[135:136, :] = jnp.where(cut, 0.0, vext[135:136, :])

    spread = jnp.concatenate([vext[7:135, :], vext[8:136, :], vext[9:137, :]], axis=1)
    hi = spread.astype(BF16)
    lo = (spread - hi.astype(F32)).astype(BF16)
    pooled = mm(hi, band[...]) + mm(lo, band[...])
    value = jnp.sum(jnp.where(in_block[...] > 0.5, pooled, 0.0), axis=0, keepdims=True) * FACTOR
    by_owner = jnp.where(iota((16, 1024), 0) == blk % OWNERS, value, 0.0).astype(BF16)
    placed = contract_last(by_owner, slot_hot[...])
    for o in range(OWNERS):
        vsend[o] = jnp.broadcast_to(placed[o : o + 1, :], (8, 128))

    def vote_copy(rel):
        return remote(vsend.at[peer(rel)], vrecv.at[me], vote_send.at[rel], vote_recv.at[rel], peer(rel))

    for rel in range(1, OWNERS):
        vote_copy(rel).start()
    vrecv[me] = vsend[me]

    out_copy.wait()
    m_all, here, there, inv = merged[0]
    merged_out = (oacc[0, 0:128, :] * here + orecv[0:128, :] * there) * inv
    by_row = merged_out.T.astype(BF16)
    for a in range(8):
        wout_ref[:, a * 128 : (a + 1) * 128] = by_row[a * WIN : (a + 1) * WIN, :]

    for copy in local_copies():
        copy.wait()
    for rel in range(1, OWNERS):
        for copy in row_copies(rel):
            copy.wait()
    for rel in range(1, OWNERS):
        remote(
            vsend.at[peer(rel)], vrecv.at[peer(OWNERS - rel)], vote_send.at[rel], vote_recv.at[rel], peer(rel)
        ).wait()
    for t in range(OWNERS):
        vstage[t // 2 : t // 2 + 1, (t % 2) * 128 : (t % 2) * 128 + 128] = vrecv[t, 0:1, :]
    vout_ref[...] = vstage[...].astype(BF16)


def on_device(window_queries, key_rows, value_rows, kept):
    vmem = pl.BlockSpec(memory_space=pltpu.VMEM)
    hbm = pl.BlockSpec(memory_space=pltpu.HBM)
    dma = pltpu.SemaphoreType.DMA
    shaped = (CHUNKS, OWNERS, BLOCK, 128)
    wout, kk, vv, votes = pl.pallas_call(
        kernel,
        out_shape=(
            jax.ShapeDtypeStruct((WIN, 1024), BF16),
            jax.ShapeDtypeStruct((8, 256, 128), BF16),
            jax.ShapeDtypeStruct((8, 256, 128), BF16),
            jax.ShapeDtypeStruct((8, 256), BF16),
        ),
        in_specs=[vmem, hbm, hbm, vmem],
        out_specs=(vmem, hbm, hbm, vmem),
        scratch_shapes=[
            pltpu.VMEM((OWNERS, CHUNKS, BLOCK, 256), BF16),
            pltpu.VMEM((CHUNKS, 144, CHUNK), BF16),
            pltpu.VMEM((2 * CHUNKS, CHUNK, ROWS), BF16),
            pltpu.VMEM((CHUNK, ROWS), F32),
            pltpu.VMEM((CHUNK, ROWS), F32),
            pltpu.VMEM((2, 128, ROWS), BF16),
            pltpu.VMEM((2, 144, ROWS), F32),
            pltpu.VMEM((144, ROWS), F32),
            pltpu.VMEM((2 * CHUNKS, 8, ROWS), F32),
            pltpu.VMEM((2, 16, ROWS), F32),
            pltpu.VMEM((2, 16, ROWS), F32),
            pltpu.VMEM((128, 128), F32),
            pltpu.VMEM((128, 1024), BF16),
            pltpu.VMEM((384, 1024), BF16),
            pltpu.VMEM((128, 1024), BF16),
            pltpu.VMEM((OWNERS, 2, 128, 128), BF16),
            pltpu.VMEM((128, 128), BF16),
            pltpu.VMEM((144, 128), F32),
            pltpu.VMEM((OWNERS, 8, 128), F32),
            pltpu.VMEM((OWNERS, 8, 128), F32),
            pltpu.VMEM((8, 256), F32),
            dma((CHUNKS,)),
            dma((CHUNKS,)),
            dma((2,)),
            dma((2, OWNERS)),
            dma((2, OWNERS)),
            dma((2,)),
            dma((2,)),
            dma((4,)),
            dma((2,)),
            dma((OWNERS,)),
            dma((OWNERS,)),
        ],
        compiler_params=pltpu.CompilerParams(
            collective_id=0, has_side_effects=True, vmem_limit_bytes=60 * 1024 * 1024
        ),
    )(window_queries, key_rows.reshape(shaped), value_rows.reshape(shaped), kept)
    return (wout, kk[None], vv[None], votes[None])


def solution(mesh):
    return jax.shard_map(
        on_device,
        mesh=mesh,
        in_specs=(P("grp", "tp"), P("tp", "grp", None), P("tp", "grp", None), P(None, "grp")),
        out_specs=(
            P("grp", "tp"),
            P("tp", None, "grp", None),
            P("tp", None, "grp", None),
            P("tp", "grp", None),
        ),
        check_vma=False,
    )
```

time: 168 us -> 52.1 us (0.31); the launches traced: 166 us -> 51.7 us
  matrix products: 50.3 us -> 0 us
  local copies, waits for them, and re-layouts: 55 us -> 6.49 us
  Pallas kernels: 0 us -> 44.6 us
  other arithmetic: 18 us -> 0 us
  waiting for transfers between devices: 17.3 us -> 0 us
  starting transfers between devices: 12.9 us -> 0 us
  loops' own time: 11.5 us -> 0 us
    dot_general x24 -> x0, matrix products: 50.3 us -> none  [the longest x16 35.9 us: scores_of(): jnp.einsum('hwd,pd->hwp', queries, key_block, preferred_element_type=jnp....]
    pallas_call x0 -> x1, Pallas kernels: none -> 44.6 us  [on_device(): pl.pallas_call(kernel, out_shape=(jax.ShapeDtypeStruct((WIN, 1024), BF16)...]
    gather x5 -> x0, local copies, waits for them, and re-layouts: 30.3 us -> none  [the longest x1 13.1 us: on_device(): pooled_rows[0][source_row]]
    ppermute x5 -> x0, waiting for transfers between devices: 15.9 us -> none  [partner(): return lax.ppermute(value, axis, pairs)]
    another operation x3 -> x0, loops' own time: 11.5 us -> none  [the longest x1 5.76 us: weight_pass(): lax.scan(weight_advance, initial, (jnp.arange(length // blk, dtype=jnp.in...]
    dynamic_slice x18 -> x0, local copies, waits for them, and re-layouts: 10.2 us -> none  [the longest x16 9.38 us: stats_pass(): lax.scan(stats_advance, initial, (jnp.arange(length // blk, dtype=jnp.int...]
    scatter x2 -> x0, local copies, waits for them, and re-layouts: 8.63 us -> none  [the longest x1 4.32 us: on_device(): jnp.zeros((owners * capacity,), jnp.int32).at[slot_of].set(local_pos)]
    reduce_sum x9 -> x0, other arithmetic: 8.26 us -> none  [the longest x8 8.23 us: stats_advance(): jnp.sum(jnp.exp(scores - new_max[..., None]), axis=-1)]
  transfers between devices with their start and end apart: 6 -> 0, of which waited for: 3 -> 0; matrix products, arithmetic and copies ran while one was open for 20% -> 0% of each run, Pallas kernels for 0% -> 0%
where the time goes in v1:
time: 52.1 us; the launch traced here: 51.7 us
  Pallas kernels  44.6 us (86%)
  local copies, waits for them, and re-layouts  6.49 us (12%)
  between operations  0.64 us (1%)
    pallas_call x1, Pallas kernels, on_device(): pl.pallas_call(kernel, out_shape=(jax.ShapeDtypeStruct((WIN, 1024), BF16)...  44.6 us
    unnamed x4, local copies, waits for them, and re-layouts  6.49 us

profile of v1, /device:TPU:224, one launch (start us, length us, event | category | flops | bytes accessed | tf_op | source)
XLA Modules:
  0.0 51.7 jit_solution(4935800562857446008)
XLA Ops:
  0.6 44.6 %shard_map.75 = (bf16[32,1024]{1,0:T(8,128)(2,1)}, bf16[8,256,128]{2,1,0:T(8,128)(2,1)}, bf16[8,256,128]{2,1,0:T(8,128)(2,1)}, bf16[8,256]{1,0:T(8,128)(2,1)}) custom-call(bf16[32,1024]{1,0:T(8,128)(2,1)} %q_ref.1, bf16[8,16,128,128]{3,2,1,0:T(8,128)(2,1)} %bitcast.5, bf16[8,16,128,128]{3,2,1,0:T(8,128)(2,1)} %bitcast.6, s32[8,2048]{1,0:T(8,128)} %kept_ref.1), custom_call_target="tpu_custom_call" | custom-call | tf_op jit(solution)/shard_map/pallas_call | solution.py:310
  45.2 1.5 %copy.12 = bf16[32,1024]{1,0:T(8,128)(2,1)} copy(bf16[32,1024]{1,0:T(8,128)(2,1)} %get-tuple-element.16) | data formatting | bytes 131072
  46.7 1.9 %copy.13 = bf16[1,8,256,128]{3,2,1,0:T(8,128)(2,1)} copy(bf16[1,8,256,128]{3,2,1,0:T(8,128)(2,1)} %bitcast.8) | data formatting | bytes 1048576
  48.6 1.9 %copy.14 = bf16[1,8,256,128]{3,2,1,0:T(8,128)(2,1)} copy(bf16[1,8,256,128]{3,2,1,0:T(8,128)(2,1)} %bitcast.7) | data formatting | bytes 1048576
  50.5 1.3 %copy.15 = bf16[1,8,256]{2,1,0:T(8,128)(2,1)} copy(bf16[1,8,256]{2,1,0:T(8,128)(2,1)} %bitcast.9) | data formatting | bytes 8192

commit v2 on v1

--- a/solution.py
+++ b/solution.py
@@ -10,6 +10,8 @@
 SEQ = 32768
 WIN = 32
 HALF = 16384
+SPLIT = 1
+FRONT = 2
 CHUNKS = 8
 OWNERS = 16
 BLOCK = 128
@@ -40,11 +42,11 @@
 
 
 def kernel(
-    q_ref, k_hbm, v_hbm, kept_ref,
+    q_hbm, k_hbm, v_hbm, kept_hbm,
     wout_ref, kk_ref, vv_ref, vout_ref,
-    kv, vt, ebuf, s_a, s_b, q_t, oacc, orecv, mrun, st_send, st_recv,
+    q_ref, kept_ref, kv, vt, ebuf, s_a, s_b, q_t, oacc, orecv, mrun, st_send, st_recv,
     slot_of, in_block, band, slot_hot, sendbuf, khalo, vext, vsend, vrecv, vstage,
-    load_k, load_v, own_sem, a2a_send, a2a_recv, q_sem, halo_sem, st_sem, o_sem, vote_send, vote_recv,
+    load_in, load_k, load_v, own_sem, a2a_send, a2a_recv, q_sem, halo_sem, st_sem, o_sem, vote_send, vote_recv,
 ):
     me = lax.axis_index("tp")
     grp = lax.axis_index("grp")
@@ -69,9 +71,15 @@
     barrier = pltpu.get_barrier_semaphore()
     for rel in range(1, OWNERS):
         pl.semaphore_signal(barrier, inc=1, device_id=(grp, peer(rel)), device_id_type=MESH)
+    kept_load = pltpu.make_async_copy(kept_hbm, kept_ref, load_in.at[0])
+    q_load = pltpu.make_async_copy(q_hbm, q_ref, load_in.at[1])
+    kept_load.start()
+    q_load.start()
     for k in range(CHUNKS):
         k_load(k).start()
         v_load(k).start()
+    kept_load.wait()
+    q_load.wait()
 
     queries = jnp.concatenate([q_ref[:, a * 128 : (a + 1) * 128] for a in range(8)], axis=0)
     q_t[0] = queries.astype(F32).T.astype(BF16)
@@ -126,65 +134,42 @@
         mrun[u] = jnp.broadcast_to(new, (8, ROWS))
         oacc[group] = oacc[group] * alpha + mm(vt[k], e)
 
-    def attend(group):
-        def ready(k):
-            if group == 0:
-                k_load(k).wait()
-                v_load(k).wait()
-
+    def ready(k):
+        k_load(k).wait()
+        v_load(k).wait()
+
+    def begin(group):
+        if group == 0:
+            ready(0)
+        return jnp.full((1, ROWS), MASKED, F32), scores(0, group, s_a)
+
+    def attend(group, first, last, carry, between):
         def step(t, carry):
             m_old, mx = carry
             k0, k1 = 2 * t, 2 * t + 1
-            ready(k1)
             if group == 0:
+                if first == 0:
+                    ready(k1)
                 transpose_values(k0)
                 transpose_values(k1)
+            between(t, 0)
             m_new = jnp.maximum(m_old, mx)
             mx1 = scores(k1, group, s_b)
             weigh(k0, group, s_a, m_old, m_new)
             m_last = jnp.maximum(m_new, mx1)
-            if group == 0:
-                @pl.when(t < CHUNKS // 2 - 1)
-                def _():
-                    ready(k0 + 2)
+            if group == 0 and first == 0:
+                ready(k0 + 2)
+            between(t, 1)
             k2 = jnp.minimum(k0 + 2, CHUNKS - 1)
             mx2 = scores(k2, group, s_a)
             weigh(k1, group, s_b, m_new, m_last)
             return m_last, mx2
 
-        ready(0)
-        mx = scores(0, group, s_a)
-        m, unused = lax.fori_loop(0, CHUNKS // 2, step, (jnp.full((1, ROWS), MASKED, F32), mx))
+        return lax.fori_loop(first, last, step, carry)
+
+    def finish(group, m):
         st_send[group, 0:8, :] = jnp.broadcast_to(m, (8, ROWS))
         st_send[group, 8:16, :] = oacc[group, 128:136, :]
-        return m
-
-    m_own = attend(0)
-
-    def pick(rel, unused):
-        o = peer(rel)
-        slot_row = iota((128, 128), 0).astype(F32)
-        hot = jnp.concatenate(
-            [as_bf16(slot_row == slot_of[pl.ds(16 * k + o, 1), :]) for k in range(CHUNKS)], axis=1
-        )
-        rows = mm(hot, kv[o].reshape(CHUNKS * 128, 256)).astype(BF16)
-        sendbuf[o, 0] = rows[:, 0:128]
-        sendbuf[o, 1] = rows[:, 128:256]
-        return unused
-
-    lax.fori_loop(0, OWNERS, pick, 0)
-
-    pl.semaphore_wait(barrier, OWNERS - 1)
-    q_copy = remote(q_t.at[0], q_t.at[1], q_sem.at[0], q_sem.at[1], mate)
-    q_copy.start()
-    edge_owner = 15 - 15 * side
-    edge_chunk = 7 - 7 * side
-    halo_copy = remote(
-        kv.at[edge_owner, edge_chunk, :, pl.ds(0, 128)], khalo, halo_sem.at[0], halo_sem.at[1], mate
-    )
-    halo_copy.start()
-    own_stat = remote(st_send.at[0], st_recv.at[0], st_sem.at[0], st_sem.at[1], mate)
-    own_stat.start()
 
     def row_copies(rel):
         o = peer(rel)
@@ -199,20 +184,63 @@
             for n, out in enumerate((kk_ref, vv_ref))
         ]
 
-    def local_copies():
-        return [
-            pltpu.make_async_copy(sendbuf.at[me, n], out.at[head, pl.ds(side * 128, 128), :], own_sem.at[n])
-            for n, out in enumerate((kk_ref, vv_ref))
-        ]
-
-    for rel in range(1, OWNERS):
-        for copy in row_copies(rel):
+    def send_rows(index):
+        for copy in row_copies(index + 1):
             copy.start()
-    for copy in local_copies():
-        copy.start()
-
+
+    def pick(rel, unused):
+        o = peer(rel)
+        slot_row = iota((128, 128), 0).astype(F32)
+        hot = jnp.concatenate(
+            [as_bf16(slot_row == slot_of[pl.ds(16 * k + o, 1), :]) for k in range(CHUNKS)], axis=1
+        )
+        rows = mm(hot, kv[o].reshape(CHUNKS * 128, 256)).astype(BF16)
+        sendbuf[o, 0] = rows[:, 0:128]
+        sendbuf[o, 1] = rows[:, 128:256]
+        return unused
+
+    def pick_four(t, unused):
+        for n in range(4):
+            pick(4 * t + n, 0)
+        return unused
+
+    carry = attend(0, 0, SPLIT, begin(0), lambda t, part: None)
+    waited = 2 * SPLIT
+    for k in range(waited + 1, CHUNKS):
+        ready(k)
+    lax.fori_loop(0, 4, pick_four, 0)
+    pl.semaphore_wait(barrier, OWNERS - 1)
+    q_copy = remote(q_t.at[0], q_t.at[1], q_sem.at[0], q_sem.at[1], mate)
+    q_copy.start()
+    edge_owner = 15 - 15 * side
+    edge_chunk = 7 - 7 * side
+    halo_copy = remote(
+        kv.at[edge_owner, edge_chunk, :, pl.ds(0, 128)], khalo, halo_sem.at[0], halo_sem.at[1], mate
+    )
+    halo_copy.start()
+    for n in range(FRONT):
+        send_rows(n)
+
+    def pace_own(t, part):
+        send_rows(FRONT + 2 * (t - SPLIT) + part)
+
+    m_own, unused = attend(0, SPLIT, CHUNKS // 2, carry, pace_own)
+    finish(0, m_own)
+    sent = FRONT + 2 * (CHUNKS // 2 - SPLIT)
+    rest = OWNERS - 1 - sent
+
+    def pace_mate(t, part):
+        index = 2 * t + part
+
+        @pl.when(index < rest)
+        def _():
+            send_rows(sent + index)
+
+    own_stat = remote(st_send.at[0], st_recv.at[0], st_sem.at[0], st_sem.at[1], mate)
+    own_stat.start()
     q_copy.wait()
-    m_mate = attend(1)
+    m_mate, unused = attend(1, 0, CHUNKS // 2, begin(1), pace_mate)
+    finish(1, m_mate)
     mate_stat = remote(st_send.at[1], st_recv.at[1], st_sem.at[2], st_sem.at[3], mate)
     mate_stat.start()
     out_copy = remote(oacc.at[1], orecv, o_sem.at[0], o_sem.at[1], mate)
@@ -233,32 +261,36 @@
         l_all = st_send[group, 8:9, :] * here + l_there * there
         merged.append((m_all, here, there, 1.0 / l_all))
 
-    row_id = iota((16, ROWS), 0)
-
-    def pieces(w):
-        hi = w.astype(BF16).astype(F32)
-        mid = (w - hi).astype(BF16).astype(F32)
-        return jnp.where(row_id == 0, hi, jnp.where(row_id == 1, mid, 0.0)).astype(BF16)
+    ones = jnp.ones((16, 128), BF16)
+
+    def spread_rows(w):
+        return jnp.broadcast_to(w, (16, ROWS)).astype(BF16)[None]
+
+    def fold(parts):
+        total = None
+        for e, w in parts:
+            product = e.reshape(e.shape[0] // 16, 16, ROWS) * w
+            both = product[:, :, 0:128] + product[:, :, 128:256]
+            total = both if total is None else total + both
+        return contract_last(ones, total.reshape(-1, 128))[0:1, :]
 
     def tally(k, unused):
-        total = jnp.zeros((16, CHUNK), F32)
+        parts = []
         for group in range(2):
             m_all, here, there, inv = merged[group]
             u = group * CHUNKS + k
-            w = jnp.exp2((mrun[u, 0:1, :] - m_all) * SCALE) * inv
-            total = total + contract_last(pieces(w), ebuf[u])
-        row = total[0:1, :] + total[1:2, :]
+            parts.append((ebuf[u], spread_rows(jnp.exp2((mrun[u, 0:1, :] - m_all) * SCALE) * inv)))
+        row = fold(parts)
         for o in range(OWNERS):
             vext[pl.ds(8 + 16 * k + o, 1), :] = row[:, o * 128 : (o + 1) * 128]
         return unused
 
     lax.fori_loop(0, CHUNKS, tally, 0)
-    halo_votes = jnp.zeros((16, 128), F32)
+    parts = []
     for group in range(2):
         m_all, here, there, inv = merged[group]
-        e = jnp.exp2(s_halo[group] * SCALE - m_all * SCALE).astype(BF16)
-        halo_votes = halo_votes + contract_last(pieces(inv), e)
-    halo_row = halo_votes[0:1, :] + halo_votes[1:2, :]
+        parts.append((jnp.exp2(s_halo[group] * SCALE - m_all * SCALE).astype(BF16), spread_rows(inv)))
+    halo_row = fold(parts)
     vext[7:8, :] = jnp.where(side == 1, halo_row, 0.0)
     vext[136:137, :] = jnp.where(side == 0, halo_row, 0.0)
     cut = jnp.logical_and(iota((1, 128), 1) >= 128 - WIN, side == 1)
@@ -280,6 +312,8 @@
     for rel in range(1, OWNERS):
         vote_copy(rel).start()
     vrecv[me] = vsend[me]
+    for n, out in enumerate((kk_ref, vv_ref)):
+        out[head, pl.ds(side * 128, 128), :] = sendbuf[me, n]
 
     out_copy.wait()
     m_all, here, there, inv = merged[0]
@@ -288,8 +322,6 @@
     for a in range(8):
         wout_ref[:, a * 128 : (a + 1) * 128] = by_row[a * WIN : (a + 1) * WIN, :]
 
-    for copy in local_copies():
-        copy.wait()
     for rel in range(1, OWNERS):
         for copy in row_copies(rel):
             copy.wait()
@@ -302,22 +334,32 @@
     vout_ref[...] = vstage[...].astype(BF16)
 
 
+def write_out(*refs):
+    copies = [pltpu.make_async_copy(refs[n], refs[4 + n], refs[8].at[n]) for n in range(4)]
+    for copy in copies:
+        copy.start()
+    for copy in copies:
+        copy.wait()
+
+
 def on_device(window_queries, key_rows, value_rows, kept):
     vmem = pl.BlockSpec(memory_space=pltpu.VMEM)
     hbm = pl.BlockSpec(memory_space=pltpu.HBM)
     dma = pltpu.SemaphoreType.DMA
     shaped = (CHUNKS, OWNERS, BLOCK, 128)
-    wout, kk, vv, votes = pl.pallas_call(
+    inside = pl.pallas_call(
         kernel,
         out_shape=(
-            jax.ShapeDtypeStruct((WIN, 1024), BF16),
-            jax.ShapeDtypeStruct((8, 256, 128), BF16),
-            jax.ShapeDtypeStruct((8, 256, 128), BF16),
-            jax.ShapeDtypeStruct((8, 256), BF16),
+            pltpu.VMEM((WIN, 1024), BF16),
+            pltpu.VMEM((8, 256, 128), BF16),
+            pltpu.VMEM((8, 256, 128), BF16),
+            pltpu.VMEM((8, 256), BF16),
         ),
-        in_specs=[vmem, hbm, hbm, vmem],
-        out_specs=(vmem, hbm, hbm, vmem),
+        in_specs=[hbm] * 4,
+        out_specs=(vmem,) * 4,
         scratch_shapes=[
+            pltpu.VMEM((WIN, 1024), BF16),
+            pltpu.VMEM((8, 2048), jnp.int32),
             pltpu.VMEM((OWNERS, CHUNKS, BLOCK, 256), BF16),
             pltpu.VMEM((CHUNKS, 144, CHUNK), BF16),
             pltpu.VMEM((2 * CHUNKS, CHUNK, ROWS), BF16),
@@ -339,6 +381,7 @@
             pltpu.VMEM((OWNERS, 8, 128), F32),
             pltpu.VMEM((OWNERS, 8, 128), F32),
             pltpu.VMEM((8, 256), F32),
+            dma((2,)),
             dma((CHUNKS,)),
             dma((CHUNKS,)),
             dma((2,)),
@@ -352,9 +395,17 @@
             dma((OWNERS,)),
         ],
         compiler_params=pltpu.CompilerParams(
-            collective_id=0, has_side_effects=True, vmem_limit_bytes=60 * 1024 * 1024
+            collective_id=0, has_side_effects=True, vmem_limit_bytes=56 * 1024 * 1024
         ),
     )(window_queries, key_rows.reshape(shaped), value_rows.reshape(shaped), kept)
+    wout, kk, vv, votes = pl.pallas_call(
+        write_out,
+        out_shape=tuple(jax.ShapeDtypeStruct(a.shape, a.dtype) for a in inside),
+        in_specs=[vmem] * 4,
+        out_specs=(hbm,) * 4,
+        scratch_shapes=[dma((4,))],
+        compiler_params=pltpu.CompilerParams(vmem_limit_bytes=1024 * 1024),
+    )(*inside)
     return (wout, kk[None], vv[None], votes[None])
 
 

time: 52.1 us -> 37.4 us (0.72)
  Pallas kernels: 44.6 us -> 36.7 us
  local copies, waits for them, and re-layouts: 6.49 us -> 0 us
    pallas_call x1 -> x2, Pallas kernels: 44.6 us -> 36.7 us  [the longest x1 35.7 us: on_device(): pl.pallas_call(kernel, out_shape=(pltpu.VMEM((WIN, 1024), BF16), pltpu.VM...]
    unnamed x4 -> x0, local copies, waits for them, and re-layouts: 6.49 us -> none
where the time goes in v2:
time: 37.4 us; the launch traced here: 37.3 us
  Pallas kernels  36.7 us (98%)
  between operations  0.64 us (2%)
    pallas_call x1, Pallas kernels, on_device(): pl.pallas_call(kernel, out_shape=(pltpu.VMEM((WIN, 1024), BF16), pltpu.VM...  35.7 us
    pallas_call x1, Pallas kernels, on_device(): pl.pallas_call(write_out, out_shape=tuple((jax.ShapeDtypeStruct(a.shape,...  1.03 us

profile of v2, /device:TPU:224, one launch (start us, length us, event | category | flops | bytes accessed | tf_op | source)
XLA Modules:
  0.0 37.3 jit_solution(16303747566201639285)
XLA Ops:
  0.6 35.7 %shard_map.75 = (bf16[32,1024]{1,0:T(8,128)(2,1)S(1)}, bf16[8,256,128]{2,1,0:T(8,128)(2,1)S(1)}, bf16[8,256,128]{2,1,0:T(8,128)(2,1)S(1)}, bf16[8,256]{1,0:T(8,128)(2,1)S(1)}) custom-call(bf16[32,1024]{1,0:T(8,128)(2,1)} %q_hbm.1, bf16[8,16,128,128]{3,2,1,0:T(8,128)(2,1)} %bitcast.5, bf16[8,16,128,128]{3,2,1,0:T(8,128)(2,1)} %bitcast.6, s32[8,2048]{1,0:T(8,128)} %kept_hbm.1), custom_call_target="tpu_custom_call" | custom-call | tf_op jit(solution)/shard_map/pallas_call | solution.py:350
  36.3 1.0 %shard_map.76 = (bf16[32,1024]{1,0:T(8,128)(2,1)}, bf16[8,256,128]{2,1,0:T(8,128)(2,1)}, bf16[8,256,128]{2,1,0:T(8,128)(2,1)}, bf16[8,256]{1,0:T(8,128)(2,1)}) custom-call(bf16[32,1024]{1,0:T(8,128)(2,1)S(1)} %get-tuple-element.12.refs_0_, bf16[8,256,128]{2,1,0:T(8,128)(2,1)S(1)} %get-tuple-element.13.refs_1_, ...), custom_call_target="tpu_custom_call" | custom-call | tf_op jit(solution)/shard_map/pallas_call | solution.py:401

commit v3 on v2

--- a/solution.py
+++ b/solution.py
@@ -11,12 +11,15 @@
 WIN = 32
 HALF = 16384
 SPLIT = 1
-FRONT = 2
+EARLY = (2, 4, 1, 3, 8, 6, 5, 7, 12, 10, 9, 11)
+LATE = (14, 13, 15)
 CHUNKS = 8
 OWNERS = 16
 BLOCK = 128
 ROWS = 256
 CHUNK = OWNERS * BLOCK
+PIECE = 256
+PIECES = CHUNK // PIECE
 SCALE = 1.4426950408889634 / 128.0**0.5
 FACTOR = (SEQ - WIN) / (7.0 * 16 * WIN)
 MASKED = -1e30
@@ -43,7 +46,7 @@
 
 def kernel(
     q_hbm, k_hbm, v_hbm, kept_hbm,
-    wout_ref, kk_ref, vv_ref, vout_ref,
+    wout_ref, rows_ref, vout_ref,
     q_ref, kept_ref, kv, vt, ebuf, s_a, s_b, q_t, oacc, orecv, mrun, st_send, st_recv,
     slot_of, in_block, band, slot_hot, sendbuf, khalo, vext, vsend, vrecv, vstage,
     load_in, load_k, load_v, own_sem, a2a_send, a2a_recv, q_sem, halo_sem, st_sem, o_sem, vote_send, vote_recv,
@@ -54,8 +57,13 @@
     head = me // 2
     mate = me + 1 - 2 * side
 
+    row, col = me // 4, me % 4
+
     def peer(rel):
-        return (me + rel) % OWNERS
+        return ((row + rel // 4) % 4) * 4 + (col + rel % 4) % 4
+
+    def source(rel):
+        return ((row + 4 - rel // 4) % 4) * 4 + (col + 4 - rel % 4) % 4
 
     def remote(src, dst, send, recv, to):
         return pltpu.make_async_remote_copy(
@@ -109,84 +117,85 @@
     hidden_row = iota((WIN, ROWS), 0) > window_of
     oacc[...] = jnp.zeros_like(oacc)
 
+    def piece_scores(j, k, group, s_ref, top):
+        keys = kv[2 * j : 2 * j + 2, k, :, 0:128].reshape(PIECE, 128)
+        s = mm(keys, q_t[group])
+        if j == PIECES - 1:
+            hide = jnp.logical_and(hidden_row, jnp.logical_and(side == 1, k == CHUNKS - 1))
+            s = jnp.concatenate([s[: PIECE - WIN], jnp.where(hide, MASKED, s[PIECE - WIN :])], axis=0)
+        s_ref[PIECE * j : PIECE * (j + 1), :] = s
+        best = jnp.max(s.reshape(PIECE // 8, 8, ROWS), axis=0)
+        return best if top is None else jnp.maximum(top, best)
+
     def scores(k, group, s_ref):
-        keys = kv[:, k, :, 0:128].reshape(CHUNK, 128)
-        s = mm(keys, q_t[group])
-        hide = jnp.logical_and(hidden_row, jnp.logical_and(side == 1, k == CHUNKS - 1))
-        last = jnp.where(hide, MASKED, s[CHUNK - WIN :])
-        s_ref[0 : CHUNK - WIN, :] = s[: CHUNK - WIN]
-        s_ref[CHUNK - WIN :, :] = last
-        return jnp.maximum(
-            jnp.max(s[: CHUNK - WIN], axis=0, keepdims=True), jnp.max(last, axis=0, keepdims=True)
-        )
+        top = None
+        for j in range(PIECES):
+            top = piece_scores(j, k, group, s_ref, top)
+        return jnp.max(top, axis=0, keepdims=True)
 
     def transpose_values(k):
         for o in range(OWNERS):
             vt[k, 0:128, o * 128 : (o + 1) * 128] = kv[o, k, :, 128:256].T
         vt[k, 128:144, :] = jnp.ones((16, CHUNK), BF16)
 
-    def weigh(k, group, s_ref, old, new):
+    def advance(k, group, s_ref, old, new, k_next, s_next, group_next):
         u = group * CHUNKS + k
-        shift = new * SCALE
-        e = jnp.exp2(s_ref[...] * SCALE - shift).astype(BF16)
-        ebuf[u] = e
-        alpha = jnp.exp2(old * SCALE - shift)
+        shift = jnp.broadcast_to(new * SCALE, (8, ROWS))
+        top = None
+        out = None
+        for j in range(PIECES):
+            if group_next is not None:
+                top = piece_scores(j, k_next, group_next, s_next, top)
+            span = slice(PIECE * j, PIECE * (j + 1))
+            s = s_ref[span, :].reshape(PIECE // 8, 8, ROWS)
+            e = jnp.exp2(s * SCALE - shift[None]).reshape(PIECE, ROWS).astype(BF16)
+            ebuf[u, span, :] = e
+            part = mm(vt[k, :, span], e)
+            out = part if out is None else out + part
+        alpha = jnp.exp2((old - new) * SCALE)
         mrun[u] = jnp.broadcast_to(new, (8, ROWS))
-        oacc[group] = oacc[group] * alpha + mm(vt[k], e)
+        oacc[group] = oacc[group] * alpha + out
+        return None if top is None else jnp.max(top, axis=0, keepdims=True)
 
     def ready(k):
         k_load(k).wait()
         v_load(k).wait()
 
-    def begin(group):
+    lowest = jnp.full((1, ROWS), MASKED, F32)
+
+    def step(group, t, carry, load, follow):
+        m_old, mx = carry
+        k0, k1 = 2 * t, 2 * t + 1
+        if load:
+            ready(k1)
         if group == 0:
-            ready(0)
-        return jnp.full((1, ROWS), MASKED, F32), scores(0, group, s_a)
-
-    def attend(group, first, last, carry, between):
-        def step(t, carry):
-            m_old, mx = carry
-            k0, k1 = 2 * t, 2 * t + 1
-            if group == 0:
-                if first == 0:
-                    ready(k1)
-                transpose_values(k0)
-                transpose_values(k1)
-            between(t, 0)
-            m_new = jnp.maximum(m_old, mx)
-            mx1 = scores(k1, group, s_b)
-            weigh(k0, group, s_a, m_old, m_new)
-            m_last = jnp.maximum(m_new, mx1)
-            if group == 0 and first == 0:
-                ready(k0 + 2)
-            between(t, 1)
-            k2 = jnp.minimum(k0 + 2, CHUNKS - 1)
-            mx2 = scores(k2, group, s_a)
-            weigh(k1, group, s_b, m_new, m_last)
-            return m_last, mx2
-
-        return lax.fori_loop(first, last, step, carry)
+            transpose_values(k0)
+            transpose_values(k1)
+        m_new = jnp.maximum(m_old, mx)
+        mx1 = advance(k0, group, s_a, m_old, m_new, k1, s_b, group)
+        m_last = jnp.maximum(m_new, mx1)
+        if load:
+            ready(k0 + 2)
+        k2 = k0 + 2 if follow == group else 0
+        mx2 = advance(k1, group, s_b, m_new, m_last, k2, s_a, follow)
+        return m_last, mx2
+
+    def attend(group, first, last, carry):
+        return lax.fori_loop(first, last, lambda t, c: step(group, t, c, False, group), carry)
 
     def finish(group, m):
         st_send[group, 0:8, :] = jnp.broadcast_to(m, (8, ROWS))
         st_send[group, 8:16, :] = oacc[group, 128:136, :]
 
-    def row_copies(rel):
+    def row_copy(rel):
         o = peer(rel)
-        return [
-            remote(
-                sendbuf.at[o, n],
-                out.at[head, pl.ds(side * 128, 128), :],
-                a2a_send.at[n, rel],
-                a2a_recv.at[n, rel],
-                o,
-            )
-            for n, out in enumerate((kk_ref, vv_ref))
-        ]
-
-    def send_rows(index):
-        for copy in row_copies(index + 1):
-            copy.start()
+        return remote(
+            sendbuf.at[o],
+            rows_ref.at[:, head, pl.ds(side * 128, 128), :],
+            a2a_send.at[rel],
+            a2a_recv.at[rel],
+            o,
+        )
 
     def pick(rel, unused):
         o = peer(rel)
@@ -204,7 +213,8 @@
             pick(4 * t + n, 0)
         return unused
 
-    carry = attend(0, 0, SPLIT, begin(0), lambda t, part: None)
+    ready(0)
+    carry = step(0, 0, (lowest, scores(0, 0, s_a)), True, 0)
     waited = 2 * SPLIT
     for k in range(waited + 1, CHUNKS):
         ready(k)
@@ -218,33 +228,24 @@
         kv.at[edge_owner, edge_chunk, :, pl.ds(0, 128)], khalo, halo_sem.at[0], halo_sem.at[1], mate
     )
     halo_copy.start()
-    for n in range(FRONT):
-        send_rows(n)
-
-    def pace_own(t, part):
-        send_rows(FRONT + 2 * (t - SPLIT) + part)
-
-    m_own, unused = attend(0, SPLIT, CHUNKS // 2, carry, pace_own)
+    for rel in EARLY:
+        row_copy(rel).start()
+
+    carry = attend(0, SPLIT, CHUNKS // 2 - 1, carry)
+    q_copy.wait()
+    m_own, mx = step(0, CHUNKS // 2 - 1, carry, False, 1)
     finish(0, m_own)
-    sent = FRONT + 2 * (CHUNKS // 2 - SPLIT)
-    rest = OWNERS - 1 - sent
-
-    def pace_mate(t, part):
-        index = 2 * t + part
-
-        @pl.when(index < rest)
-        def _():
-            send_rows(sent + index)
-
     own_stat = remote(st_send.at[0], st_recv.at[0], st_sem.at[0], st_sem.at[1], mate)
+    carry = attend(1, 0, CHUNKS // 2 - 1, (lowest, mx))
     own_stat.start()
-    q_copy.wait()
-    m_mate, unused = attend(1, 0, CHUNKS // 2, begin(1), pace_mate)
+    m_mate, unused = step(1, CHUNKS // 2 - 1, carry, False, None)
     finish(1, m_mate)
     mate_stat = remote(st_send.at[1], st_recv.at[1], st_sem.at[2], st_sem.at[3], mate)
     mate_stat.start()
     out_copy = remote(oacc.at[1], orecv, o_sem.at[0], o_sem.at[1], mate)
     out_copy.start()
+    for rel in LATE:
+        row_copy(rel).start()
     halo_copy.wait()
     s_halo = [mm(khalo[...], q_t[group]) for group in range(2)]
     own_stat.wait()
@@ -285,7 +286,12 @@
             vext[pl.ds(8 + 16 * k + o, 1), :] = row[:, o * 128 : (o + 1) * 128]
         return unused
 
-    lax.fori_loop(0, CHUNKS, tally, 0)
+    def tally_four(t, unused):
+        for n in range(4):
+            tally(4 * t + n, 0)
+        return unused
+
+    lax.fori_loop(0, CHUNKS // 4, tally_four, 0)
     parts = []
     for group in range(2):
         m_all, here, there, inv = merged[group]
@@ -312,8 +318,8 @@
     for rel in range(1, OWNERS):
         vote_copy(rel).start()
     vrecv[me] = vsend[me]
-    for n, out in enumerate((kk_ref, vv_ref)):
-        out[head, pl.ds(side * 128, 128), :] = sendbuf[me, n]
+    for n in range(2):
+        rows_ref[n, head, pl.ds(side * 128, 128), :] = sendbuf[me, n]
 
     out_copy.wait()
     m_all, here, there, inv = merged[0]
@@ -323,19 +329,19 @@
         wout_ref[:, a * 128 : (a + 1) * 128] = by_row[a * WIN : (a + 1) * WIN, :]
 
     for rel in range(1, OWNERS):
-        for copy in row_copies(rel):
-            copy.wait()
+        row_copy(rel).wait()
     for rel in range(1, OWNERS):
         remote(
-            vsend.at[peer(rel)], vrecv.at[peer(OWNERS - rel)], vote_send.at[rel], vote_recv.at[rel], peer(rel)
+            vsend.at[peer(rel)], vrecv.at[source(rel)], vote_send.at[rel], vote_recv.at[rel], peer(rel)
         ).wait()
     for t in range(OWNERS):
         vstage[t // 2 : t // 2 + 1, (t % 2) * 128 : (t % 2) * 128 + 128] = vrecv[t, 0:1, :]
     vout_ref[...] = vstage[...].astype(BF16)
 
 
-def write_out(*refs):
-    copies = [pltpu.make_async_copy(refs[n], refs[4 + n], refs[8].at[n]) for n in range(4)]
+def write_out(wout, rows, votes, wout_hbm, kk_hbm, vv_hbm, votes_hbm, sems):
+    pairs = ((rows.at[0], kk_hbm), (rows.at[1], vv_hbm), (wout, wout_hbm), (votes, votes_hbm))
+    copies = [pltpu.make_async_copy(src, dst, sems.at[n]) for n, (src, dst) in enumerate(pairs)]
     for copy in copies:
         copy.start()
     for copy in copies:
@@ -351,12 +357,11 @@
         kernel,
         out_shape=(
             pltpu.VMEM((WIN, 1024), BF16),
-            pltpu.VMEM((8, 256, 128), BF16),
-            pltpu.VMEM((8, 256, 128), BF16),
+            pltpu.VMEM((2, 8, 256, 128), BF16),
             pltpu.VMEM((8, 256), BF16),
         ),
         in_specs=[hbm] * 4,
-        out_specs=(vmem,) * 4,
+        out_specs=(vmem,) * 3,
         scratch_shapes=[
             pltpu.VMEM((WIN, 1024), BF16),
             pltpu.VMEM((8, 2048), jnp.int32),
@@ -385,8 +390,8 @@
             dma((CHUNKS,)),
             dma((CHUNKS,)),
             dma((2,)),
-            dma((2, OWNERS)),
-            dma((2, OWNERS)),
+            dma((OWNERS,)),
+            dma((OWNERS,)),
             dma((2,)),
             dma((2,)),
             dma((4,)),
@@ -400,8 +405,13 @@
     )(window_queries, key_rows.reshape(shaped), value_rows.reshape(shaped), kept)
     wout, kk, vv, votes = pl.pallas_call(
         write_out,
-        out_shape=tuple(jax.ShapeDtypeStruct(a.shape, a.dtype) for a in inside),
-        in_specs=[vmem] * 4,
+        out_shape=(
+            jax.ShapeDtypeStruct((WIN, 1024), BF16),
+            jax.ShapeDtypeStruct((8, 256, 128), BF16),
+            jax.ShapeDtypeStruct((8, 256, 128), BF16),
+            jax.ShapeDtypeStruct((8, 256), BF16),
+        ),
+        in_specs=[vmem] * 3,
         out_specs=(hbm,) * 4,
         scratch_shapes=[dma((4,))],
         compiler_params=pltpu.CompilerParams(vmem_limit_bytes=1024 * 1024),

time: 37.4 us -> 33.3 us (0.89)
  Pallas kernels: 36.7 us -> 32.5 us
    pallas_call x1, Pallas kernels: 35.7 us -> 31.5 us  [on_device(): pl.pallas_call(kernel, out_shape=(pltpu.VMEM((WIN, 1024), BF16), pltpu.VM...]
where the time goes in v3:
time: 33.3 us; the launch traced here: 33.2 us
  Pallas kernels  32.5 us (98%)
  between operations  0.64 us (2%)
    pallas_call x1, Pallas kernels, on_device(): pl.pallas_call(kernel, out_shape=(pltpu.VMEM((WIN, 1024), BF16), pltpu.VM...  31.5 us
    pallas_call x1, Pallas kernels, on_device(): pl.pallas_call(write_out, out_shape=(jax.ShapeDtypeStruct((WIN, 1024), BF...  1.01 us

profile of v3, /device:TPU:224, one launch (start us, length us, event | category | flops | bytes accessed | tf_op | source)
XLA Modules:
  0.0 33.2 jit_solution(12341747993215172863)
XLA Ops:
  0.6 31.5 %shard_map.75 = (bf16[32,1024]{1,0:T(8,128)(2,1)S(1)}, bf16[2,8,256,128]{3,2,1,0:T(8,128)(2,1)S(1)}, bf16[8,256]{1,0:T(8,128)(2,1)S(1)}) custom-call(bf16[32,1024]{1,0:T(8,128)(2,1)} %q_hbm.1, bf16[8,16,128,128]{3,2,1,0:T(8,128)(2,1)} %bitcast.5, bf16[8,16,128,128]{3,2,1,0:T(8,128)(2,1)} %bitcast.6, s32[8,2048]{1,0:T(8,128)} %kept_hbm.1), custom_call_target="tpu_custom_call" | custom-call | tf_op jit(solution)/shard_map/pallas_call | solution.py:356
  32.2 1.0 %shard_map.76 = (bf16[32,1024]{1,0:T(8,128)(2,1)}, bf16[8,256,128]{2,1,0:T(8,128)(2,1)}, bf16[8,256,128]{2,1,0:T(8,128)(2,1)}, bf16[8,256]{1,0:T(8,128)(2,1)}) custom-call(bf16[32,1024]{1,0:T(8,128)(2,1)S(1)} %get-tuple-element.11.wout, bf16[2,8,256,128]{3,2,1,0:T(8,128)(2,1)S(1)} %get-tuple-element.12.rows, bf16[8,256]{1,0:T(8,128)(2,1)S(1)} %get-tuple-element.13.votes), custom_call_target="tpu_custom_call" | custom-call | tf_op jit(solution)/shard_map/pallas_call | solution.py:406

commit v4 on v3

--- a/solution.py
+++ b/solution.py
@@ -10,7 +10,6 @@
 SEQ = 32768
 WIN = 32
 HALF = 16384
-SPLIT = 1
 EARLY = (2, 4, 1, 3, 8, 6, 5, 7, 12, 10, 9, 11)
 LATE = (14, 13, 15)
 CHUNKS = 8
@@ -76,6 +75,7 @@
     def v_load(k):
         return pltpu.make_async_copy(v_hbm.at[k], kv.at[:, k, :, pl.ds(128, 128)], load_v.at[k])
 
+    khalo[...] = jnp.zeros_like(khalo)
     barrier = pltpu.get_barrier_semaphore()
     for rel in range(1, OWNERS):
         pl.semaphore_signal(barrier, inc=1, device_id=(grp, peer(rel)), device_id_type=MESH)
@@ -163,25 +163,21 @@
 
     lowest = jnp.full((1, ROWS), MASKED, F32)
 
-    def step(group, t, carry, load, follow):
+    def step(group, t, carry, follow):
         m_old, mx = carry
         k0, k1 = 2 * t, 2 * t + 1
-        if load:
-            ready(k1)
         if group == 0:
             transpose_values(k0)
             transpose_values(k1)
         m_new = jnp.maximum(m_old, mx)
         mx1 = advance(k0, group, s_a, m_old, m_new, k1, s_b, group)
         m_last = jnp.maximum(m_new, mx1)
-        if load:
-            ready(k0 + 2)
         k2 = k0 + 2 if follow == group else 0
         mx2 = advance(k1, group, s_b, m_new, m_last, k2, s_a, follow)
         return m_last, mx2
 
     def attend(group, first, last, carry):
-        return lax.fori_loop(first, last, lambda t, c: step(group, t, c, False, group), carry)
+        return lax.fori_loop(first, last, lambda t, c: step(group, t, c, group), carry)
 
     def finish(group, m):
         st_send[group, 0:8, :] = jnp.broadcast_to(m, (8, ROWS))
@@ -214,9 +210,8 @@
         return unused
 
     ready(0)
-    carry = step(0, 0, (lowest, scores(0, 0, s_a)), True, 0)
-    waited = 2 * SPLIT
-    for k in range(waited + 1, CHUNKS):
+    first = scores(0, 0, s_a)
+    for k in range(1, CHUNKS):
         ready(k)
     lax.fori_loop(0, 4, pick_four, 0)
     pl.semaphore_wait(barrier, OWNERS - 1)
@@ -224,29 +219,37 @@
     q_copy.start()
     edge_owner = 15 - 15 * side
     edge_chunk = 7 - 7 * side
-    halo_copy = remote(
-        kv.at[edge_owner, edge_chunk, :, pl.ds(0, 128)], khalo, halo_sem.at[0], halo_sem.at[1], mate
-    )
-    halo_copy.start()
+    edge_row = 112 - 112 * side
+
+    def halo(to_row):
+        return remote(
+            kv.at[edge_owner, edge_chunk, pl.ds(edge_row, 16), pl.ds(0, 128)],
+            khalo.at[pl.ds(to_row, 16), :],
+            halo_sem.at[0],
+            halo_sem.at[1],
+            mate,
+        )
+
+    halo(edge_row).start()
     for rel in EARLY:
         row_copy(rel).start()
 
-    carry = attend(0, SPLIT, CHUNKS // 2 - 1, carry)
+    carry = attend(0, 0, CHUNKS // 2 - 1, (lowest, first))
     q_copy.wait()
-    m_own, mx = step(0, CHUNKS // 2 - 1, carry, False, 1)
+    m_own, mx = step(0, CHUNKS // 2 - 1, carry, 1)
     finish(0, m_own)
     own_stat = remote(st_send.at[0], st_recv.at[0], st_sem.at[0], st_sem.at[1], mate)
     carry = attend(1, 0, CHUNKS // 2 - 1, (lowest, mx))
     own_stat.start()
-    m_mate, unused = step(1, CHUNKS // 2 - 1, carry, False, None)
+    m_mate, unused = step(1, CHUNKS // 2 - 1, carry, None)
     finish(1, m_mate)
     mate_stat = remote(st_send.at[1], st_recv.at[1], st_sem.at[2], st_sem.at[3], mate)
     mate_stat.start()
-    out_copy = remote(oacc.at[1], orecv, o_sem.at[0], o_sem.at[1], mate)
+    out_copy = remote(oacc.at[1, pl.ds(0, 128), :], orecv, o_sem.at[0], o_sem.at[1], mate)
     out_copy.start()
     for rel in LATE:
         row_copy(rel).start()
-    halo_copy.wait()
+    halo(112 * side).wait()
     s_halo = [mm(khalo[...], q_t[group]) for group in range(2)]
     own_stat.wait()
     mate_stat.wait()
@@ -297,8 +300,9 @@
         m_all, here, there, inv = merged[group]
         parts.append((jnp.exp2(s_halo[group] * SCALE - m_all * SCALE).astype(BF16), spread_rows(inv)))
     halo_row = fold(parts)
-    vext[7:8, :] = jnp.where(side == 1, halo_row, 0.0)
-    vext[136:137, :] = jnp.where(side == 0, halo_row, 0.0)
+    along = iota((1, 128), 1)
+    vext[7:8, :] = jnp.where(jnp.logical_and(side == 1, along >= 125), halo_row, 0.0)
+    vext[136:137, :] = jnp.where(jnp.logical_and(side == 0, along < 3), halo_row, 0.0)
     cut = jnp.logical_and(iota((1, 128), 1) >= 128 - WIN, side == 1)
     vext[135:136, :] = jnp.where(cut, 0.0, vext[135:136, :])
 
@@ -323,7 +327,7 @@
 
     out_copy.wait()
     m_all, here, there, inv = merged[0]
-    merged_out = (oacc[0, 0:128, :] * here + orecv[0:128, :] * there) * inv
+    merged_out = (oacc[0, 0:128, :] * here + orecv[...] * there) * inv
     by_row = merged_out.T.astype(BF16)
     for a in range(8):
         wout_ref[:, a * 128 : (a + 1) * 128] = by_row[a * WIN : (a + 1) * WIN, :]
@@ -372,7 +376,7 @@
             pltpu.VMEM((CHUNK, ROWS), F32),
             pltpu.VMEM((2, 128, ROWS), BF16),
             pltpu.VMEM((2, 144, ROWS), F32),
-            pltpu.VMEM((144, ROWS), F32),
+            pltpu.VMEM((128, ROWS), F32),
             pltpu.VMEM((2 * CHUNKS, 8, ROWS), F32),
             pltpu.VMEM((2, 16, ROWS), F32),
             pltpu.VMEM((2, 16, ROWS), F32),

time: 33.3 us -> 32.5 us (0.976)
  Pallas kernels: 32.5 us -> 31.8 us
    pallas_call x1, Pallas kernels: 31.5 us -> 30.8 us  [on_device(): pl.pallas_call(kernel, out_shape=(pltpu.VMEM((WIN, 1024), BF16), pltpu.VM...]
where the time goes in v4:
time: 32.5 us; the launch traced here: 32.4 us
  Pallas kernels  31.8 us (98%)
  between operations  0.64 us (2%)
    pallas_call x1, Pallas kernels, on_device(): pl.pallas_call(kernel, out_shape=(pltpu.VMEM((WIN, 1024), BF16), pltpu.VM...  30.8 us
    pallas_call x1, Pallas kernels, on_device(): pl.pallas_call(write_out, out_shape=(jax.ShapeDtypeStruct((WIN, 1024), BF...  1.01 us

profile of v4, /device:TPU:224, one launch (start us, length us, event | category | flops | bytes accessed | tf_op | source)
XLA Modules:
  0.0 32.4 jit_solution(2100230586907264272)
XLA Ops:
  0.6 30.8 %shard_map.75 = (bf16[32,1024]{1,0:T(8,128)(2,1)S(1)}, bf16[2,8,256,128]{3,2,1,0:T(8,128)(2,1)S(1)}, bf16[8,256]{1,0:T(8,128)(2,1)S(1)}) custom-call(bf16[32,1024]{1,0:T(8,128)(2,1)} %q_hbm.1, bf16[8,16,128,128]{3,2,1,0:T(8,128)(2,1)} %bitcast.5, bf16[8,16,128,128]{3,2,1,0:T(8,128)(2,1)} %bitcast.6, s32[8,2048]{1,0:T(8,128)} %kept_hbm.1), custom_call_target="tpu_custom_call" | custom-call | tf_op jit(solution)/shard_map/pallas_call | solution.py:360
  31.4 1.0 %shard_map.76 = (bf16[32,1024]{1,0:T(8,128)(2,1)}, bf16[8,256,128]{2,1,0:T(8,128)(2,1)}, bf16[8,256,128]{2,1,0:T(8,128)(2,1)}, bf16[8,256]{1,0:T(8,128)(2,1)}) custom-call(bf16[32,1024]{1,0:T(8,128)(2,1)S(1)} %get-tuple-element.11.wout, bf16[2,8,256,128]{3,2,1,0:T(8,128)(2,1)S(1)} %get-tuple-element.12.rows, bf16[8,256]{1,0:T(8,128)(2,1)S(1)} %get-tuple-element.13.votes), custom_call_target="tpu_custom_call" | custom-call | tf_op jit(solution)/shard_map/pallas_call | solution.py:410
